TPU v7x, 128 devices: a whole 4x4x4 slice. The times are simulated.
128 devices in a mesh: dp: 128 (over x, y, z, core).
Axes of the slice: x: 4, y: 4, z: 4, core: 2. Of those that a mesh axis runs over, the one named last changes fastest.
Arguments:
- features: bfloat16 [131072, 3136], P('dp'), may hold values from -6 to 6
- w_one: bfloat16 [512, 3136], replicated, may hold values from -0.109375 to 0.109375
- b_one: float32 [512], replicated, may hold values from -3 to 3
- w_two: bfloat16 [512, 918], replicated, may hold values from -0.25 to 0.25
- b_two: float32 [918], replicated, may hold values from -112 to 112
- action: int32 [131072], P('dp'), may hold values from 0 to 17
- target_probs: float32 [131072, 18, 51], P('dp'), may hold values from 0 to 1, as said below
- next_action: int32 [131072], P('dp'), may hold values from 0 to 17
- lower_idx: int32 [131072, 51], P('dp'), may hold values from 0 to 49
- upper_frac: float32 [131072, 51], P('dp'), may hold values from 0 to 1
- is_weight: float32 [131072], P('dp'), may hold values from 0.1 to 1
Outputs:
- grad_w1: float32 [512, 3136], replicated
- grad_b1: float32 [512], replicated
- grad_w2: float32 [512, 918], replicated
- grad_b2: float32 [918], replicated
- mean_loss: float32 [], replicated
- priorities: float32 [131072], P('dp')
Inputs may be any that keep to these rules, and one draw needn't show every extreme that they name: Each target_probs[i, a] is a distribution over the atoms: positive entries that sum to one.
All inputs are finite; a program needn't handle non-finite values.
Results may differ from a plain program's by a relative error of at most 0.005.
Values sent between devices are 32-bit elements; how exact they have to be, the bound alone decides.
A program may use at most 128 MiB of HBM per device.

v0:
```python
import jax
import jax.numpy as jnp
from jax import lax
from jax.sharding import PartitionSpec as P


def forward_loss(
    features,
    w_one,
    b_one,
    w_two,
    b_two,
    action,
    target_probs,
    next_action,
    lower_idx,
    upper_frac,
    is_weight,
):
    row_count = features.shape[0]
    n_act = target_probs.shape[1]
    n_atom = target_probs.shape[2]
    pre_act = (
        lax.dot_general(
            features, w_one, (((1,), (1,)), ((), ())), preferred_element_type=jnp.float32
        )
        + b_one
    )
    hidden = jnp.maximum(pre_act, 0.0).astype(jnp.bfloat16)
    logits = (jnp.dot(hidden, w_two, preferred_element_type=jnp.float32) + b_two).reshape(
        row_count, n_act, n_atom
    )
    chosen = jnp.take_along_axis(logits, action[:, None, None], axis=1)[:, 0, :]
    log_probs = jax.nn.log_softmax(chosen, axis=-1)
    next_probs = jnp.take_along_axis(target_probs, next_action[:, None, None], axis=1)[:, 0, :]
    atom_ids = jnp.arange(n_atom, dtype=jnp.int32)
    mass_low = next_probs * (1.0 - upper_frac)
    mass_high = next_probs * upper_frac
    low_hot = lower_idx[:, :, None] == atom_ids[None, None, :]
    high_hot = lower_idx[:, :, None] + 1 == atom_ids[None, None, :]
    projected = jnp.sum(
        jnp.where(low_hot, mass_low[:, :, None], 0.0)
        + jnp.where(high_hot, mass_high[:, :, None], 0.0),
        axis=1,
    )
    cross_ent = -jnp.sum(projected * log_probs, axis=-1)
    grad_chosen = is_weight[:, None] * (
        jnp.exp(log_probs) * jnp.sum(projected, axis=-1, keepdims=True) - projected
    )
    act_hot = action[:, None] == jnp.arange(n_act, dtype=jnp.int32)[None, :]
    grad_logits = (
        jnp.where(act_hot[:, :, None], grad_chosen[:, None, :], 0.0)
        .reshape(row_count, n_act * n_atom)
        .astype(jnp.bfloat16)
    )
    grad_hidden = lax.dot_general(
        grad_logits, w_two, (((1,), (1,)), ((), ())), preferred_element_type=jnp.float32
    )
    grad_pre = jnp.where(pre_act > 0.0, grad_hidden, 0.0).astype(jnp.bfloat16)
    return (hidden, grad_logits, grad_pre, cross_ent)


def on_device(
    features,
    w_one,
    b_one,
    w_two,
    b_two,
    action,
    target_probs,
    next_action,
    lower_idx,
    upper_frac,
    is_weight,
):
    total_rows = features.shape[0] * lax.axis_size("dp")
    hidden, grad_logits, grad_pre, cross_ent = forward_loss(
        features,
        w_one,
        b_one,
        w_two,
        b_two,
        action,
        target_probs,
        next_action,
        lower_idx,
        upper_frac,
        is_weight,
    )
    local_loss = jnp.sum(is_weight * cross_ent)
    local_top = jnp.max(cross_ent)
    loss_sum = lax.psum(local_loss, "dp")
    top = lax.pmax(local_top, "dp")
    local_w2 = lax.dot_general(
        hidden, grad_logits, (((0,), (0,)), ((), ())), preferred_element_type=jnp.float32
    )
    local_b2 = jnp.sum(grad_logits.astype(jnp.float32), axis=0)
    local_b1 = jnp.sum(grad_pre.astype(jnp.float32), axis=0)
    grad_b1, grad_w2, grad_b2 = lax.psum((local_b1, local_w2, local_b2), "dp")
    local_w1 = lax.dot_general(
        grad_pre, features, (((0,), (0,)), ((), ())), preferred_element_type=jnp.float32
    )
    grad_w1 = lax.psum(local_w1, "dp")
    priorities = cross_ent / jnp.maximum(top, 1.0)
    mean_loss = loss_sum / total_rows
    return (grad_w1, grad_b1, grad_w2, grad_b2, mean_loss, priorities)


def solution(mesh):
    in_specs = (
        P("dp", None),
        P(),
        P(),
        P(),
        P(),
        P("dp"),
        P("dp", None, None),
        P("dp"),
        P("dp", None),
        P("dp", None),
        P("dp"),
    )
    out_specs = (P(), P(), P(), P(), P(), P("dp"))
    return jax.shard_map(
        on_device, mesh=mesh, in_specs=in_specs, out_specs=out_specs, check_vma=False
    )
```

profile of v0, /device:TPU:1, one launch (start us, length us, event | category | flops | bytes accessed | tf_op | source)
XLA Modules:
  0.0 265.4 jit_solution(11242338552301293826)
XLA Ops:
  7.2 0.0 copy-start
  7.2 0.0 all-reduce.4.cloned.1.call-start
  7.2 0.9 and_reduce_fusion
  8.1 0.8 iota_compare_fusion.2
  8.9 0.7 and_reduce_fusion.1
  9.6 1.0 broadcast_add_fusion
  10.5 0.0 copy-done
  10.5 0.0 copy-start.7
  10.6 0.0 copy-start.8
  10.6 0.0 copy-start.9
  10.6 5.9 %fusion.16 = f32[1024,512]{1,0:T(8,128)S(1)} fusion(bf16[1024,3136]{0,1:T(8,128)(2,1)} %param.13, bf16[512,3136]{0,1:T(8,128)(2,1)S(1)} %copy-done), kind=kOutput, calls=%fused_computation.50 | convolution fusion | flops 3288334336 | bytes 11730944 | tf_op jit(solution)/shard_map/dot_general | solution.py:24
  16.5 0.0 copy-start.10
  16.5 1.3 copy-done.10
  17.8 0.0 copy-done.7
  17.8 0.0 copy-done.8
  17.8 0.0 copy-done.9
  17.8 3.0 %convolution_add_fusion = f32[1024,918]{0,1:T(8,128)} fusion(bf16[512,918]{0,1:T(8,128)(2,1)S(1)} %copy-done.7, f32[918]{0:T(1024)S(1)} %copy-done.8, f32[1024,512]{1,0:T(8,128)S(1)} %fusion.16, f32[512]{0:T(512)S(1)} %copy-done.9), kind=kOutput, calls=%fused_computation.12 | convolution fusion | flops 965105664 | bytes 6803032 | tf_op jit(solution)/shard_map/dot_general | solution.py:30
  20.8 3.9 %reshape.118 = f32[1024,18,51]{0,2,1:T(8,128)} reshape(f32[1024,918]{0,1:T(8,128)} %convolution_add_fusion) | data formatting | bytes 7520256 | tf_op jit(solution)/shard_map/reshape | solution.py:30
  24.7 7.5 %copy.39 = f32[1024,18,51]{2,0,1:T(8,128)} copy(f32[1024,18,51]{0,2,1:T(8,128)} %reshape.118) | data formatting | bytes 7520256 | tf_op jit(solution)/shard_map/reshape | solution.py:30
  32.2 10.6 %gather_fusion = f32[1024,51]{1,0:T(8,128)S(1)} fusion(f32[1024,18,51]{2,0,1:T(8,128)} %copy.39, s32[1024]{0:T(1024)S(1)} %bitcast.54), kind=kCustom, calls=%fused_computation.clone | custom fusion | bytes 425984 | tf_op jit(solution)/shard_map/jit(take_along_axis)/gather | solution.py:33
  42.8 0.4 fusion.4
  43.2 0.5 exponential_reduce_fusion
  43.7 7.5 %copy.40 = f32[1024,18,51]{2,0,1:T(8,128)} copy(f32[1024,18,51]{0,2,1:T(8,128)} %param.19) | data formatting | bytes 7520256 | tf_op args[6]
  51.2 10.5 %gather_fusion.1 = f32[1024,51]{1,0:T(8,128)S(1)} fusion(f32[1024,18,51]{2,0,1:T(8,128)} %copy.40, s32[1024]{0:T(1024)S(1)} %bitcast.53), kind=kCustom, calls=%fused_computation.1.clone | custom fusion | bytes 425984 | tf_op jit(solution)/shard_map/jit(take_along_axis)/gather | solution.py:35
  61.7 0.0 copy-start.6
  61.7 0.2 copy.41
  61.9 0.0 copy-done.5
  62.0 4.5 %fusion.1 = (f32[1024]{0:T(1024)S(1)}, f32[1024,51]{0,1:T(8,128)S(1)}) fusion(f32[1024,51]{0,1:T(8,128)S(1)} %get-tuple-element.21, s32[1024,51]{0,1:T(8,128)S(1)} %broadcast_add_fusion, f32[1024,51]{0,1:T(8,128)S(1)} %get-tuple-element.20, s32[1024,51]{0,1:T(8,128)S(1)} %copy-done.4), kind=kLoop, calls=%fused_computation.5 | loop fusion | flops 18590720 | bytes 1048576 | tf_op jit(solution)/shard_map/reduce_sum | solution.py:48
  66.5 0.2 copy.42
  66.7 1.1 fusion.3
  67.7 0.2 copy.43
  67.9 0.4 select_convert_fusion
  68.3 1.8 convert_element_type.22
  70.1 3.9 %convert_reduce_fusion.1 = (f32[512]{0:T(512)S(1)}, bf16[1024,512]{1,0:T(8,128)(2,1)S(1)}) fusion(bf16[1024,918]{0,1:T(8,128)(2,1)} %convert_element_type.22, bf16[512,918]{0,1:T(8,128)(2,1)} %param.16, f32[1024,512]{1,0:T(8,128)} %copy-done.10, f32[512]{0:T(512)S(1)} %copy-done.9), kind=kOutput, calls=%fused_computation.9 | convolution fusion | flops 965737984 | bytes 5969920 | tf_op jit(solution)/shard_map/dot_general | solution.py:56
  74.1 2.4 fusion.5
  76.5 8.2 %fusion.17 = f32[512,3136]{0,1:T(8,128)} fusion(bf16[1024,3136]{0,1:T(8,128)(2,1)} %param.13, bf16[1024,512]{1,0:T(8,128)(2,1)S(1)} %get-tuple-element.25), kind=kOutput, calls=%fused_computation.51 | convolution fusion | flops 3288334336 | bytes 13893632 | tf_op jit(solution)/shard_map/dot_general | solution.py:100
  84.7 0.0 all-reduce.4.cloned.1.call-update
  84.7 0.6 multiply_reduce_fusion
  85.3 0.6 negate_reduce_fusion
  85.9 69.2 %pmax.7 = f32[]{:T(128)} all-reduce(f32[]{:T(128)} %get-tuple-element.9), channel_id=1, replica_groups=mesh['dp'=128] {'dp'}, use_global_device_ids=true, to_apply=%region_14.16 | all-reduce | flops 1 | bytes 8 | tf_op jit(solution)/shard_map/pmax | solution.py:93
  155.1 0.5 convert_reduce_fusion
  155.6 0.1 reduce_sum.74
  156.3 63.0 %all-reduce = (f32[512]{0:T(512)}, f32[918]{0:T(1024)}, f32[]{:T(128)}) all-reduce(f32[512]{0:T(512)S(1)} %get-tuple-element.24, f32[918]{0:T(1024)S(1)} %reduce_sum.74, f32[]{:T(128)} %get-tuple-element.10), channel_id=1, replica_groups=mesh['dp'=128] {'dp'}, use_global_device_ids=true, to_apply=%region_6.8 | all-reduce | flops 1431 | bytes 11448 | tf_op jit(solution)/shard_map/psum | solution.py:99
  220.0 0.6 negate_divide_fusion
  220.6 29.1 %all-reduce.4.cloned.1.call-done = (f32[512,3136]{0,1:T(8,128)}, f32[512,918]{0,1:T(8,128)}) async-done(((f32[512,3136]{0,1:T(8,128)}, f32[512,918]{0,1:T(8,128)}), (f32[512,3136]{0,1:T(8,128)}, f32[512,918]{0,1:T(8,128)})) %all-reduce.4.cloned.1.call-update) | async-done | bytes 8302608 | tf_op jit(solution)/shard_map/psum | solution.py:103
  249.7 6.5 %copy.47 = f32[512,3136]{0,1:T(8,128)} copy(f32[512,3136]{0,1:T(8,128)} %get-tuple-element.28) | data formatting | bytes 12845056
  256.2 0.0 copy-done.2
  256.2 1.2 copy.48
  (16 shorter events, 0.1 us)
Async XLA Ops:
  7.2 3.4 %copy-start = (bf16[512,3136]{0,1:T(8,128)(2,1)S(1)}, bf16[512,3136]{0,1:T(8,128)(2,1)}, u32[]{:S(2)}) copy-start(bf16[512,3136]{0,1:T(8,128)(2,1)} %param.14) | copy-start | bytes 9633796
  7.2 242.5 %all-reduce.4.cloned.1.call-start = ((), (), s32[]{:S(2)}) async-start(), calls=%async_computation | async-start | bytes 16613376 | tf_op jit(solution)/shard_map/psum | solution.py:103
  10.5 7.3 %copy-start.7 = (bf16[512,918]{0,1:T(8,128)(2,1)S(1)}, bf16[512,918]{0,1:T(8,128)(2,1)}, u32[]{:S(2)}) copy-start(bf16[512,918]{0,1:T(8,128)(2,1)} %param.16) | copy-start | bytes 2820100
  10.6 7.3 %copy-start.8 = (f32[918]{0:T(1024)S(1)}, f32[918]{0:T(1024)}, u32[]{:S(2)}) copy-start(f32[918]{0:T(1024)} %param.17) | copy-start | bytes 11020
  10.6 7.2 %copy-start.9 = (f32[512]{0:T(512)S(1)}, f32[512]{0:T(512)}, u32[]{:S(2)}) copy-start(f32[512]{0:T(512)} %param.15) | copy-start | bytes 6148
  16.5 1.3 copy-start.10
  51.2 10.7 %copy-start.5 = (f32[1024,51]{0,1:T(8,128)S(1)}, f32[1024,51]{0,1:T(8,128)}, u32[]{:S(2)}) copy-start(f32[1024,51]{0,1:T(8,128)} %param.22) | copy-start | bytes 626692
  51.2 10.8 %copy-start.4 = (s32[1024,51]{0,1:T(8,128)S(1)}, s32[1024,51]{0,1:T(8,128)}, u32[]{:S(2)}) copy-start(s32[1024,51]{0,1:T(8,128)} %param.21) | copy-start | bytes 626692
  61.7 5.0 %copy-start.6 = (f32[1024]{0:T(1024)S(1)}, f32[1024]{0:T(1024)}, u32[]{:S(2)}) copy-start(f32[1024]{0:T(1024)} %param.23) | copy-start | bytes 12292
  70.1 3.9 %copy-start.3 = (bf16[1024,918]{0,1:T(8,128)(2,1)S(1)}, bf16[1024,918]{0,1:T(8,128)(2,1)}, u32[]{:S(2)}) copy-start(bf16[1024,918]{0,1:T(8,128)(2,1)} %convert_element_type.22) | copy-start | bytes 5640196
  70.1 3.9 %copy-start.11 = (f32[1024,512]{1,0:T(8,128)S(1)}, f32[1024,512]{1,0:T(8,128)}, u32[]{:S(2)}) copy-start(f32[1024,512]{1,0:T(8,128)} %copy-done.10) | copy-start | bytes 6291460
  249.7 6.5 %copy-start.2 = (f32[512,918]{0,1:T(8,128)S(1)}, f32[512,918]{0,1:T(8,128)}, u32[]{:S(2)}) copy-start(f32[512,918]{0,1:T(8,128)} %get-tuple-element.30) | copy-start | bytes 5640196
  249.7 7.7 %copy-start.1 = (bf16[512,3136]{0,1:T(8,128)(2,1)S(1)}, bf16[512,3136]{0,1:T(8,128)(2,1)}, u32[]{:S(2)}) copy-start(bf16[512,3136]{0,1:T(8,128)(2,1)} %param.14) | copy-start | bytes 9633796
Sparse Core Ops, SparseCore 0:
  84.8 164.8 all-reduce.3
where the time goes:
time: 266 us; the launch traced here: 265 us
  blocking collectives  132 us (50%)
  local copies, waits for them, and re-layouts  51.4 us (19%)
  waiting for transfers between devices  29.2 us (11%)
  matrix products  23.5 us (9%)
  between operations  16.7 us (6%)
  other arithmetic  12.5 us (5%)
    pmax x1, blocking collectives, on_device(): top = lax.pmax(local_top, 'dp')  69.2 us
    psum x1, blocking collectives, on_device(): grad_b1, grad_w2, grad_b2 = lax.psum((local_b1, local_w2, local_b2), 'dp')  63 us
    psum x1, waiting for transfers between devices, on_device(): grad_w1 = lax.psum(local_w1, 'dp')  29.1 us
    unnamed x27, local copies, waits for them, and re-layouts  16.6 us
    reshape x2, local copies, waits for them, and re-layouts, forward_loss(): (jnp.dot(hidden, w_two, preferred_element_type=jnp.float32) + b_two).resh...  11.3 us
    gather x2, local copies, waits for them, and re-layouts, forward_loss(): jnp.take_along_axis(target_probs, next_action[:, None, None], axis=1)  10.7 us
    gather x1, local copies, waits for them, and re-layouts, forward_loss(): chosen = jnp.take_along_axis(logits, action[:, None, None], axis=1)[:, 0, :]  10.6 us
    dot_general x1, matrix products, on_device(): lax.dot_general(grad_pre, features, (((0,), (0,)), ((), ())), preferred_e...  8.19 us
  transfers between devices with their start and end apart: 1, of which 1 were waited for; matrix products, arithmetic and copies ran while one was open for 1% of the time, Pallas kernels for 0%

commit v1 on v0

v1 whole, which is shorter than its diff:
```python
import functools

import jax
import jax.numpy as jnp
from jax import lax
from jax.experimental import pallas as pl
from jax.experimental.pallas import tpu as pltpu
from jax.sharding import PartitionSpec as P

MESH = pl.DeviceIdType.MESH
F32, BF16 = jnp.float32, jnp.bfloat16

FEAT, HID, ACT, ATOM, ROWS = 3136, 512, 18, 51, 1024
SLOT = 64
HEAD = ACT * SLOT
HEADS = ACT * ATOM

W2_AT = FEAT
B1_AT = W2_AT + HEADS
B2_AT = B1_AT + 1
TOP_AT = B2_AT + 2
LOSS_AT = TOP_AT + 1
TOTAL_ROWS = 4096
HALF = TOTAL_ROWS // 2
STREAMS = ((0, 640), (640, 640), (1280, 768))


def compute_kernel(
    feat_hbm, w1_hbm, b1_hbm, w2_hbm, b2_hbm, act_hbm, tp_hbm, nact_hbm, low_hbm, frac_hbm, isw_hbm,
    part_ref, ce_ref,
    feat, w1, b1_ref, w2raw, b2_ref, act_ref, tp, nact_ref, low_ref, frac_ref, isw_ref,
    w2f, w2p, b2col, mlow, mhigh, proj, hid, glt, gp, gb2, sems,
):
    me = lax.axis_index("dp")
    pairs = [
        (w2_hbm, w2raw), (b2_hbm, b2_ref), (nact_hbm, nact_ref), (low_hbm, low_ref), (frac_hbm, frac_ref),
        (tp_hbm, tp), (w1_hbm, w1), (b1_hbm, b1_ref), (feat_hbm, feat), (act_hbm, act_ref), (isw_hbm, isw_ref),
    ]
    copies = [pltpu.make_async_copy(src, dst, sems.at[i]) for i, (src, dst) in enumerate(pairs)]
    for copy in copies:
        copy.start()

    copies[0].wait()
    copies[1].wait()
    w2f[...] = w2raw[...].astype(F32)
    wrow = lax.broadcasted_iota(jnp.int32, (SLOT, HID), 0)
    for a in range(ACT):
        if a < ACT - 1:
            block = w2f[ATOM * a : ATOM * a + SLOT, :]
        else:
            block = jnp.concatenate([w2f[ATOM * a : HEADS, :], jnp.zeros((SLOT - ATOM, HID), F32)], axis=0)
        w2p[SLOT * a : SLOT * (a + 1), :] = jnp.where(wrow < ATOM, block, 0.0).astype(BF16)
    b2row = jnp.concatenate([b2_ref[...], jnp.zeros((1, 1024 - HEADS), F32)], axis=1)
    b2col[0:1024, :] = jnp.broadcast_to(b2row, (128, 1024)).T
    b2col[1024:, :] = jnp.zeros((64, 128), F32)

    for copy in copies[2:6]:
        copy.wait()
    atom_row = lax.broadcasted_iota(jnp.int32, (SLOT, 128), 0)

    def project(t, carry):
        lanes = pl.ds(pl.multiple_of(t * 128, 128), 128)
        nact = nact_ref[:, lanes]
        probs = jnp.zeros((ATOM, 128), F32)
        for a in range(ACT):
            probs = jnp.where(nact == a, tp[a, :, lanes], probs)
        frac = frac_ref[:, lanes]
        mlow[...] = probs * (1.0 - frac)
        mhigh[...] = probs * frac
        low_sum = jnp.zeros((SLOT, 128), F32)
        high_sum = jnp.zeros((SLOT, 128), F32)
        for j in range(ATOM):
            hot = low_ref[pl.ds(j, 1), lanes] == atom_row
            low_sum = low_sum + jnp.where(hot, mlow[pl.ds(j, 1), :], 0.0)
            high_sum = high_sum + jnp.where(hot, mhigh[pl.ds(j, 1), :], 0.0)
        high_sum = jnp.where(atom_row == 0, 0.0, pltpu.roll(high_sum, 1, 0))
        proj[:, lanes] = low_sum + high_sum
        return carry

    lax.fori_loop(0, ROWS // 128, project, 0)

    for copy in copies[6:]:
        copy.wait()

    def forward(t, carry):
        cols = pl.ds(pl.multiple_of(t * 256, 256), 256)
        pre = lax.dot_general(feat[:, cols], w1[...], (((0,), (0,)), ((), ())), preferred_element_type=F32)
        hid[cols, :] = jnp.maximum(pre + b1_ref[...], 0.0).astype(BF16)
        return carry

    lax.fori_loop(0, ROWS // 256, forward, 0)

    valid = lax.broadcasted_iota(jnp.int32, (SLOT, 256), 0) < ATOM

    def head(t, carry):
        loss, top = carry
        cols = pl.ds(pl.multiple_of(t * 256, 256), 256)
        logits = lax.dot_general(w2p[...], hid[cols, :], (((1,), (1,)), ((), ())), preferred_element_type=F32)
        action = act_ref[:, cols]
        chosen = jnp.zeros((SLOT, 256), F32)
        for a in range(ACT):
            bias = b2col[ATOM * a : ATOM * a + SLOT, :]
            biased = logits[SLOT * a : SLOT * (a + 1), :] + jnp.concatenate([bias, bias], axis=1)
            chosen = jnp.where(action == a, biased, chosen)
        chosen = jnp.where(valid, chosen, -1e30)
        shifted = chosen - jnp.max(chosen, axis=0, keepdims=True)
        expd = jnp.where(valid, jnp.exp(shifted), 0.0)
        log_probs = shifted - jnp.log(jnp.sum(expd, axis=0, keepdims=True))
        projected = proj[:, cols]
        cross = -jnp.sum(jnp.where(valid, projected * log_probs, 0.0), axis=0, keepdims=True)
        weight = isw_ref[:, cols]
        probs = jnp.where(valid, jnp.exp(log_probs), 0.0)
        grad = weight * (probs * jnp.sum(projected, axis=0, keepdims=True) - projected)
        grad16 = grad.astype(BF16)
        for a in range(ACT):
            glt[SLOT * a : SLOT * (a + 1), cols] = jnp.where(action == a, grad, 0.0).astype(BF16)
        ce_ref[:, cols] = cross
        return loss + weight * cross, jnp.maximum(top, cross)

    loss_row, top_row = lax.fori_loop(
        0, ROWS // 256, head, (jnp.zeros((1, 256), F32), jnp.full((1, 256), -jnp.inf, F32))
    )

    def back(t, gb1):
        cols = pl.ds(pl.multiple_of(t * 256, 256), 256)
        gh = lax.dot_general(glt[:, cols], w2p[...], (((0,), (0,)), ((), ())), preferred_element_type=F32)
        g16 = jnp.where(hid[cols, :].astype(F32) > 0.0, gh, 0.0).astype(BF16)
        gp[cols, :] = g16
        return gb1 + jnp.sum(g16.astype(F32), axis=0, keepdims=True)

    gb1 = lax.fori_loop(0, ROWS // 256, back, jnp.zeros((1, HID), F32))

    group = 6
    for g in range(ACT // group):
        rows = group * SLOT
        gl = glt[g * rows : (g + 1) * rows, :]
        gw2 = lax.dot_general(gl, hid[...], (((1,), (0,)), ((), ())), preferred_element_type=F32)
        for i in range(group):
            a = g * group + i
            part_ref[W2_AT + ATOM * a : W2_AT + ATOM * (a + 1), :] = gw2[SLOT * i : SLOT * i + ATOM, :]
            ga = glt[SLOT * a : SLOT * (a + 1), :].astype(F32)
            gb2[ATOM * a : ATOM * (a + 1), :] = jnp.broadcast_to(jnp.sum(ga, axis=1, keepdims=True), (SLOT, 128))[:ATOM]
    gb2[HEADS:, :] = jnp.zeros((1024 - HEADS, 128), F32)
    gb2_row = gb2[...].T[0:1, :]

    lane = lax.broadcasted_iota(jnp.int32, (1, HID), 1)
    top = jnp.max(top_row)
    loss = jnp.sum(loss_row)
    tail = jnp.concatenate(
        [
            gb1,
            gb2_row[:, :HID],
            gb2_row[:, HID:],
            jnp.where(lane == me, top, 0.0),
            jnp.where(lane == 0, loss, 0.0),
            jnp.zeros((TOTAL_ROWS - LOSS_AT - 1, HID), F32),
        ],
        axis=0,
    )
    part_ref[B1_AT:, :] = tail

    def grad_w1(i, carry):
        rows = pl.ds(pl.multiple_of(i * 448, 64), 448)
        part_ref[rows, :] = jnp.dot(feat[rows, :], gp[...], preferred_element_type=F32)
        return carry

    lax.fori_loop(0, FEAT // 448, grad_w1, 0)


def compute(feat, w1, b1, w2, b2, action, tp, naction, low, frac, isw):
    any_spec = pl.BlockSpec(memory_space=pltpu.HBM)
    vm = pl.BlockSpec(memory_space=pltpu.VMEM)
    return pl.pallas_call(
        compute_kernel,
        name="compute",
        in_specs=[any_spec] * 11,
        out_specs=[vm, vm],
        out_shape=[pltpu.VMEM((TOTAL_ROWS, HID), F32), pltpu.VMEM((1, ROWS), F32)],
        scratch_shapes=[
            pltpu.VMEM((FEAT, ROWS), BF16),
            pltpu.VMEM((FEAT, HID), BF16),
            pltpu.VMEM((1, HID), F32),
            pltpu.VMEM((HEADS, HID), BF16),
            pltpu.VMEM((1, HEADS), F32),
            pltpu.VMEM((1, ROWS), jnp.int32),
            pltpu.VMEM((ACT, ATOM, ROWS), F32),
            pltpu.VMEM((1, ROWS), jnp.int32),
            pltpu.VMEM((ATOM, ROWS), jnp.int32),
            pltpu.VMEM((ATOM, ROWS), F32),
            pltpu.VMEM((1, ROWS), F32),
            pltpu.VMEM((HEADS, HID), F32),
            pltpu.VMEM((HEAD, HID), BF16),
            pltpu.VMEM((1088, 128), F32),
            pltpu.VMEM((ATOM, 128), F32),
            pltpu.VMEM((ATOM, 128), F32),
            pltpu.VMEM((SLOT, ROWS), F32),
            pltpu.VMEM((ROWS, HID), BF16),
            pltpu.VMEM((HEAD, ROWS), BF16),
            pltpu.VMEM((ROWS, HID), BF16),
            pltpu.VMEM((1024, 128), F32),
            pltpu.SemaphoreType.DMA((11,)),
        ],
        compiler_params=pltpu.CompilerParams(vmem_limit_bytes=45 * 1024 * 1024),
    )(feat, w1, b1, w2, b2, action, tp, naction, low, frac, isw)


class Sends:
    def __init__(self, send_sem, recv_sem):
        self.send_sem, self.recv_sem, self.made = send_sem, recv_sem, []

    def __call__(self, src, dst, device):
        i = len(self.made)
        copy = pltpu.make_async_remote_copy(
            src_ref=src, dst_ref=dst, send_sem=self.send_sem.at[i], recv_sem=self.recv_sem.at[i],
            device_id=(device,), device_id_type=MESH,
        )
        copy.start()
        self.made.append(copy)
        return copy


COPIES = 3 * 38
LO, HI = slice(0, HID // 2), slice(HID // 2, HID)


def rows_at(start, size):
    return pl.ds(pl.multiple_of(start, 8), size)


def plan(me, core):
    out = []
    for s in range(3):
        stages = []
        for k in range(3):
            axis = (s + k + core) % 3
            stride = 32 - 33 * axis + 9 * axis * axis
            at = (me // stride) % 4
            ahead = [me + stride * ((at + d) % 4 - at) for d in range(4)]
            stages.append((at, ahead))
        out.append(stages)
    return out


def comm_kernel(part, ce, tot, prio, work, plus_a, minus_a, one_a, plus_b, minus_b, one_b, piece, send_sem, recv_sem):
    me = lax.axis_index("dp")
    core = me % 2
    sibling = me + 1 - 2 * core
    mine, theirs = plan(me, core), plan(me, 1 - core)
    near = [sibling]
    for k in range(3):
        near += mine[0][k][1][1:]
    barrier = pltpu.get_barrier_semaphore()
    for device in near:
        pl.semaphore_signal(barrier, inc=1, device_id=(device,), device_id_type=MESH)
    pl.semaphore_wait(barrier, len(near))

    send = Sends(send_sem, recv_sem)
    base = core * HALF
    other = (1 - core) * HALF
    ORDER = (2, 1, 3, 0)

    swap = {}
    for d in ORDER:
        for s, (first, size) in enumerate(STREAMS):
            q = size // 4
            at = (theirs[s][0][0] + d) % 4 * q + first
            swap[s, d] = send(part.at[rows_at(other + at, q), :], work.at[rows_at(at, q), :], sibling)

    def scatter(k, blocks, sizes, plus, minus, one, before=None):
        copies, quarter = {}, {}
        for d in ORDER:
            for s in range(3):
                at, ahead = mine[s][k]
                q = sizes[s]
                rows = rows_at(blocks[s] + (at + d) % 4 * q, q)
                quarter[s, d] = rows
                if before is not None:
                    before(s, d, rows)
                here = pl.ds(0, q)
                if d == 2:
                    copies[s, "p1"] = send(work.at[rows, LO], one.at[s, here, LO], ahead[1])
                    copies[s, "m1"] = send(work.at[rows, HI], one.at[s, here, HI], ahead[3])
                elif d == 1:
                    copies[s, "p2"] = send(work.at[rows, HI], plus.at[s, here, HI], ahead[1])
                elif d == 3:
                    copies[s, "m2"] = send(work.at[rows, LO], minus.at[s, here, LO], ahead[3])
        for s in range(3):
            at, ahead = mine[s][k]
            here = pl.ds(0, sizes[s])
            copies[s, "p1"].wait_recv()
            rows = quarter[s, 1]
            work[rows, LO] = work[rows, LO] + one[s, here, LO]
            copies[s, "p3"] = send(work.at[rows, LO], plus.at[s, here, LO], ahead[1])
            copies[s, "m1"].wait_recv()
            rows = quarter[s, 3]
            work[rows, HI] = work[rows, HI] + one[s, here, HI]
            copies[s, "m3"] = send(work.at[rows, HI], minus.at[s, here, HI], ahead[3])
        for s in range(3):
            here = pl.ds(0, sizes[s])
            for name in ("p2", "m2", "p3", "m3"):
                copies[s, name].wait_recv()
            rows = quarter[s, 0]
            work[rows, :] = work[rows, :] + (plus[s, here, :] + minus[s, here, :])
        return [blocks[s] + mine[s][k][0] * sizes[s] for s in range(3)]

    def add_own(s, d, rows):
        q = STREAMS[s][1] // 4
        at = (mine[s][0][0] + d) % 4 * q + STREAMS[s][0]
        swap[s, d].wait_recv()
        work[rows, :] = work[rows, :] + part[rows_at(base + at, q), :]

    size_a = [size // 4 for _, size in STREAMS]
    size_b = [size // 16 for _, size in STREAMS]
    block_a = [first for first, _ in STREAMS]
    block_b = scatter(0, block_a, size_a, plus_a, minus_a, one_a, add_own)
    block_c = scatter(1, block_b, size_b, plus_b, minus_b, one_b)

    def lanes_at(p):
        return pl.ds(pl.multiple_of(p * 128, 128), 128)

    last = {}
    for d in (2, 1, 3):
        for s in range(3):
            at, ahead = mine[s][2]
            last[s, d] = send(
                work.at[rows_at(block_c[s], size_b[s]), lanes_at((at + d) % 4)],
                piece.at[s, d - 1, pl.ds(0, size_b[s]), :], ahead[d],
            )
    final = {}
    for s in range(3):
        at, ahead = mine[s][2]
        here = pl.ds(0, size_b[s])
        for d in (1, 3, 2):
            last[s, d].wait_recv()
        got = work[rows_at(block_c[s], size_b[s]), lanes_at(at)] + (piece[s, 0, here, :] + piece[s, 2, here, :])
        rows = rows_at(base + block_c[s], size_b[s])
        tot[rows, lanes_at(at)] = got + piece[s, 1, here, :]
        for d in (2, 1, 3):
            ref = tot.at[rows, lanes_at(at)]
            final[s, d] = send(ref, ref, ahead[d])
    for s in range(3):
        for d in (1, 3, 2):
            final[s, d].wait_recv()

    def gather(k, blocks, sizes, pair):
        copies, pairs = {}, []

        def rows_of(s, d):
            return rows_at(base + blocks[s] + (mine[s][k][0] + d) % 4 * sizes[s], sizes[s])

        def put(s, d, lanes, device):
            ref = tot.at[rows_of(s, d), lanes]
            return send(ref, ref, device)

        def to_sibling(s, d):
            if pair:
                pairs.append(put(s, d, slice(0, HID), sibling))

        for s in range(3):
            ahead = mine[s][k][1]
            copies[s, "p1"] = put(s, 0, LO, ahead[1])
            copies[s, "m1"] = put(s, 0, HI, ahead[3])
            copies[s, "p2"] = put(s, 0, HI, ahead[1])
            copies[s, "m2"] = put(s, 0, LO, ahead[3])
        for s in range(3):
            to_sibling(s, 0)
        for s in range(3):
            ahead = mine[s][k][1]
            copies[s, "p1"].wait_recv()
            copies[s, "p3"] = put(s, 3, LO, ahead[1])
            copies[s, "m1"].wait_recv()
            copies[s, "m3"] = put(s, 1, HI, ahead[3])
        for s in range(3):
            copies[s, "p2"].wait_recv()
            to_sibling(s, 3)
            copies[s, "m2"].wait_recv()
            to_sibling(s, 1)
        for s in range(3):
            copies[s, "p3"].wait_recv()
            copies[s, "m3"].wait_recv()
            to_sibling(s, 2)
        for copy in pairs:
            copy.wait_recv()

    gather(1, block_b, size_b, False)
    gather(0, block_a, size_a, True)
    for copy in send.made:
        copy.wait_send()
    top = jnp.max(tot[TOP_AT : TOP_AT + 1, 0:128])
    prio[...] = ce[...] / jnp.maximum(top, 1.0)


def all_sum(part, ce):
    vm = pl.BlockSpec(memory_space=pltpu.VMEM)
    q = STREAMS[2][1] // 4
    return pl.pallas_call(
        comm_kernel,
        name="all_sum",
        in_specs=[vm, vm],
        out_specs=[vm, vm],
        out_shape=[pltpu.VMEM((TOTAL_ROWS, HID), F32), pltpu.VMEM((1, ROWS), F32)],
        scratch_shapes=[
            pltpu.VMEM((HALF, HID), F32),
            pltpu.VMEM((3, q, HID), F32),
            pltpu.VMEM((3, q, HID), F32),
            pltpu.VMEM((3, q, HID), F32),
            pltpu.VMEM((3, q // 4, HID), F32),
            pltpu.VMEM((3, q // 4, HID), F32),
            pltpu.VMEM((3, q // 4, HID), F32),
            pltpu.VMEM((3, 3, q // 4, 128), F32),
            pltpu.SemaphoreType.DMA((COPIES,)),
            pltpu.SemaphoreType.DMA((COPIES,)),
        ],
        compiler_params=pltpu.CompilerParams(
            vmem_limit_bytes=16 * 1024 * 1024, collective_id=0, has_side_effects=True
        ),
    )(part, ce)


def on_device(features, w_one, b_one, w_two, b_two, action, target_probs, next_action, lower_idx, upper_frac, is_weight):
    part, ce = compute(
        features.T, w_one.T, b_one[None, :], w_two.T, b_two[None, :], action[None, :],
        target_probs.transpose(1, 2, 0), next_action[None, :], lower_idx.T, upper_frac.T, is_weight[None, :],
    )
    total, prio = all_sum(part, ce)
    return (
        total[:FEAT].T,
        total[B1_AT],
        total[W2_AT:B1_AT].T,
        total[B2_AT : B2_AT + 2].reshape(-1)[:HEADS],
        total[LOSS_AT, 0] / (ROWS * lax.axis_size("dp")),
        prio[0],
    )


def solution(mesh):
    in_specs = (
        P("dp", None), P(), P(), P(), P(), P("dp"), P("dp", None, None), P("dp"), P("dp", None), P("dp", None), P("dp"),
    )
    out_specs = (P(), P(), P(), P(), P(), P("dp"))
    return jax.shard_map(on_device, mesh=mesh, in_specs=in_specs, out_specs=out_specs, check_vma=False)
```

time: 266 us -> 99.2 us (0.37)
  blocking collectives: 132 us -> 0 us
  Pallas kernels: 0 us -> 84 us
  local copies, waits for them, and re-layouts: 51.4 us -> 12.5 us
  waiting for transfers between devices: 29.2 us -> 0 us
  matrix products: 23.5 us -> 0 us
  between operations: 16.7 us -> 2.45 us
  other arithmetic: 12.5 us -> 0 us
    pallas_call x0 -> x2, Pallas kernels: none -> 84 us  [the longest x1 63 us: all_sum(): pl.pallas_call(comm_kernel, name='all_sum', in_specs=[vm, vm], out_specs=...]
    pmax x1 -> x0, blocking collectives: 69.2 us -> none  [on_device(): top = lax.pmax(local_top, 'dp')]
    psum x1 -> x0, blocking collectives: 63 us -> none  [on_device(): grad_b1, grad_w2, grad_b2 = lax.psum((local_b1, local_w2, local_b2), 'dp')]
    psum x1 -> x0, waiting for transfers between devices: 29.1 us -> none  [on_device(): grad_w1 = lax.psum(local_w1, 'dp')]
    dot_general x5 -> x0, matrix products: 23.5 us -> none  [the longest x1 8.19 us: on_device(): lax.dot_general(grad_pre, features, (((0,), (0,)), ((), ())), preferred_e...]
    gather x3 -> x0, local copies, waits for them, and re-layouts: 21.3 us -> none  [the longest x2 10.7 us: forward_loss(): jnp.take_along_axis(target_probs, next_action[:, None, None], axis=1)]
    reshape x2 -> x0, local copies, waits for them, and re-layouts: 11.3 us -> none  [forward_loss(): (jnp.dot(hidden, w_two, preferred_element_type=jnp.float32) + b_two).resh...]
    unnamed x27 -> x17, local copies, waits for them, and re-layouts: 16.6 us -> 6.49 us
  transfers between devices with their start and end apart: 1 -> 0, of which waited for: 1 -> 0; matrix products, arithmetic and copies ran while one was open for 1% -> 0% of each run, Pallas kernels for 0% -> 0%
where the time goes in v1:
time: 99.2 us; the launch traced here: 98.9 us
  Pallas kernels  84 us (85%)
  local copies, waits for them, and re-layouts  12.5 us (13%)
  between operations  2.45 us (2%)
    pallas_call x1, Pallas kernels, all_sum(): pl.pallas_call(comm_kernel, name='all_sum', in_specs=[vm, vm], out_specs=...  63 us
    pallas_call x1, Pallas kernels, compute(): pl.pallas_call(compute_kernel, name='compute', in_specs=[any_spec] * 11,...  21 us
    unnamed x17, local copies, waits for them, and re-layouts  6.49 us
    transpose x1, local copies, waits for them, and re-layouts, on_device(): total[:FEAT]  3.47 us

profile of v1, /device:TPU:1, one launch (start us, length us, event | category | flops | bytes accessed | tf_op | source)
XLA Modules:
  0.0 98.9 jit_solution(14609357350506385563)
XLA Ops:
  0.6 0.0 copy-start
  0.6 0.9 copy-done
  1.6 0.0 copy-start.1
  1.6 0.9 copy-done.1
  2.5 0.0 copy-start.2
  2.5 0.7 copy-done.2
  3.2 0.0 copy-start.3
  3.2 0.7 copy-done.3
  3.9 0.0 copy-start.4
  3.9 0.7 copy-done.4
  4.6 0.0 copy-start.5
  4.6 0.7 copy-done.5
  5.3 0.0 copy-start.6
  5.3 0.7 copy-done.6
  5.9 21.0 %compute.1 = (f32[4096,512]{1,0:T(8,128)S(1)}, f32[1,1024]{1,0:T(1,128)S(1)}) custom-call(bf16[3136,1024]{1,0:T(8,128)(2,1)} %bitcast.30, bf16[3136,512]{1,0:T(8,128)(2,1)} %bitcast.32, f32[1,512]{1,0:T(1,128)S(1)} %bitcast.29, bf16[918,512]{1,0:T(8,128)(2,1)} %bitcast.33, f32[1,918]{1,0:T(1,128)S(1)} %bitcast.25, s32[1,1024]{1,0:T(1,128)S(1)} %bitcast.26, ...), custom_call_target="tpu_custom_call" | custom-call | tf_op jit(solution)/shard_map/compute/pallas_call | solution.py:173
  26.9 63.0 %all_sum.1 = (f32[4096,512]{1,0:T(8,128)S(1)}, f32[1,1024]{1,0:T(1,128)S(1)}) custom-call(f32[4096,512]{1,0:T(8,128)S(1)} %get-tuple-element.10.part, f32[1,1024]{1,0:T(1,128)S(1)} %get-tuple-element.11.ce), custom_call_target="tpu_custom_call" | custom-call | tf_op jit(solution)/shard_map/all_sum/pallas_call | solution.py:396
  90.0 0.5 slice.23
  91.1 0.6 copy.19
  91.7 0.6 slice.19
  92.3 0.6 copy.17
  92.9 1.4 %slice_bitcast_fusion.1 = f32[512,918]{0,1:T(8,128)} fusion(f32[4096,512]{1,0:T(8,128)S(1)} %get-tuple-element.12), kind=kLoop, calls=%fused_computation.1 | loop fusion | bytes 3760128 | tf_op jit(solution)/shard_map/transpose | solution.py:429
  94.3 3.5 %slice_bitcast_fusion = f32[512,3136]{0,1:T(8,128)} fusion(f32[4096,512]{1,0:T(8,128)S(1)} %get-tuple-element.12), kind=kLoop, calls=%fused_computation | loop fusion | bytes 12845056 | tf_op jit(solution)/shard_map/transpose | solution.py:427
  (1 shorter events, 0.0 us)
Async XLA Ops:
  0.6 0.9 copy-start
  1.6 0.9 copy-start.1
  2.5 0.7 copy-start.2
  3.2 0.7 copy-start.3
  3.9 0.7 copy-start.4
  4.6 0.7 copy-start.5
  5.3 0.7 copy-start.6

commit v2 on v1

v2 whole, which is shorter than its diff:
```python
import functools

import jax
import jax.numpy as jnp
from jax import lax
from jax.experimental import pallas as pl
from jax.experimental.pallas import tpu as pltpu
from jax.sharding import PartitionSpec as P

MESH = pl.DeviceIdType.MESH
F32, BF16 = jnp.float32, jnp.bfloat16

FEAT, HID, ACT, ATOM, ROWS = 3136, 512, 18, 51, 1024
SLOT = 64
HEAD = ACT * SLOT
HEADS = ACT * ATOM

W1_AT = 928
B1_AT = W1_AT + FEAT
B2_AT = B1_AT + 1
TOP_AT = B2_AT + 2
LOSS_AT = TOP_AT + 1
TOTAL_ROWS = 4096
WAVES = ((128, 128, 128), (256, 256, 256), (256, 256, 384))


def main_kernel(
    feat_hbm, w1_hbm, b1_hbm, w2_hbm, b2_hbm, act_hbm, tp_hbm, nact_hbm, low_hbm, frac_hbm, isw_hbm,
    tot, ce_ref,
    feat, w1, b1_ref, w2raw, b2_ref, act_ref, tp, nact_ref, low_ref, frac_ref, isw_ref,
    w2f, w2p, b2col, mlow, mhigh, proj, hid, glt, gp, gb2, part_ref, sems, send_sem, recv_sem, *buffers,
):
    me = lax.axis_index("dp")
    core = me % 2
    sibling = me + 1 - 2 * core
    pairs = [
        (w2_hbm, w2raw), (b2_hbm, b2_ref), (nact_hbm, nact_ref), (low_hbm, low_ref), (frac_hbm, frac_ref),
        (tp_hbm, tp), (w1_hbm, w1), (b1_hbm, b1_ref), (feat_hbm, feat), (act_hbm, act_ref), (isw_hbm, isw_ref),
    ]
    copies = [pltpu.make_async_copy(src, dst, sems.at[i]) for i, (src, dst) in enumerate(pairs)]
    for copy in copies:
        copy.start()
    near = [sibling]
    for axis in range(3):
        near += ring(me, axis)[1][1:]
    barrier = pltpu.get_barrier_semaphore()
    for device in near:
        pl.semaphore_signal(barrier, inc=1, device_id=(device,), device_id_type=MESH)

    copies[0].wait()
    copies[1].wait()
    w2f[...] = w2raw[...].astype(F32)
    wrow = lax.broadcasted_iota(jnp.int32, (SLOT, HID), 0)
    for a in range(ACT):
        if a < ACT - 1:
            block = w2f[ATOM * a : ATOM * a + SLOT, :]
        else:
            block = jnp.concatenate([w2f[ATOM * a : HEADS, :], jnp.zeros((SLOT - ATOM, HID), F32)], axis=0)
        w2p[SLOT * a : SLOT * (a + 1), :] = jnp.where(wrow < ATOM, block, 0.0).astype(BF16)
    b2row = jnp.concatenate([b2_ref[...], jnp.zeros((1, 1024 - HEADS), F32)], axis=1)
    b2col[0:1024, :] = jnp.broadcast_to(b2row, (128, 1024)).T
    b2col[1024:, :] = jnp.zeros((64, 128), F32)

    for copy in copies[2:6]:
        copy.wait()
    atom_row = lax.broadcasted_iota(jnp.int32, (SLOT, 128), 0)

    def project(t, carry):
        lanes = pl.ds(pl.multiple_of(t * 128, 128), 128)
        nact = nact_ref[:, lanes]
        probs = jnp.zeros((ATOM, 128), F32)
        for a in range(ACT):
            probs = jnp.where(nact == a, tp[a, :, lanes], probs)
        frac = frac_ref[:, lanes]
        mlow[...] = probs * (1.0 - frac)
        mhigh[...] = probs * frac
        low_sum = jnp.zeros((SLOT, 128), F32)
        high_sum = jnp.zeros((SLOT, 128), F32)
        for j in range(ATOM):
            hot = low_ref[pl.ds(j, 1), lanes] == atom_row
            low_sum = low_sum + jnp.where(hot, mlow[pl.ds(j, 1), :], 0.0)
            high_sum = high_sum + jnp.where(hot, mhigh[pl.ds(j, 1), :], 0.0)
        high_sum = jnp.where(atom_row == 0, 0.0, pltpu.roll(high_sum, 1, 0))
        proj[:, lanes] = low_sum + high_sum
        return carry

    lax.fori_loop(0, ROWS // 128, project, 0)

    for copy in copies[6:]:
        copy.wait()

    def forward(t, carry):
        cols = pl.ds(pl.multiple_of(t * 256, 256), 256)
        pre = lax.dot_general(feat[:, cols], w1[...], (((0,), (0,)), ((), ())), preferred_element_type=F32)
        hid[cols, :] = jnp.maximum(pre + b1_ref[...], 0.0).astype(BF16)
        return carry

    lax.fori_loop(0, ROWS // 256, forward, 0)

    valid = lax.broadcasted_iota(jnp.int32, (SLOT, 256), 0) < ATOM

    def head(t, carry):
        loss, top = carry
        cols = pl.ds(pl.multiple_of(t * 256, 256), 256)
        logits = lax.dot_general(w2p[...], hid[cols, :], (((1,), (1,)), ((), ())), preferred_element_type=F32)
        action = act_ref[:, cols]
        chosen = jnp.zeros((SLOT, 256), F32)
        for a in range(ACT):
            bias = b2col[ATOM * a : ATOM * a + SLOT, :]
            biased = logits[SLOT * a : SLOT * (a + 1), :] + jnp.concatenate([bias, bias], axis=1)
            chosen = jnp.where(action == a, biased, chosen)
        chosen = jnp.where(valid, chosen, -1e30)
        shifted = chosen - jnp.max(chosen, axis=0, keepdims=True)
        expd = jnp.where(valid, jnp.exp(shifted), 0.0)
        log_probs = shifted - jnp.log(jnp.sum(expd, axis=0, keepdims=True))
        projected = proj[:, cols]
        cross = -jnp.sum(jnp.where(valid, projected * log_probs, 0.0), axis=0, keepdims=True)
        weight = isw_ref[:, cols]
        probs = jnp.where(valid, jnp.exp(log_probs), 0.0)
        grad = weight * (probs * jnp.sum(projected, axis=0, keepdims=True) - projected)
        grad16 = grad.astype(BF16)
        for a in range(ACT):
            glt[SLOT * a : SLOT * (a + 1), cols] = jnp.where(action == a, grad, 0.0).astype(BF16)
        ce_ref[:, cols] = cross
        return loss + weight * cross, jnp.maximum(top, cross)

    loss_row, top_row = lax.fori_loop(
        0, ROWS // 256, head, (jnp.zeros((1, 256), F32), jnp.full((1, 256), -jnp.inf, F32))
    )

    group = 6
    for g in range(ACT // group):
        rows = group * SLOT
        gl = glt[g * rows : (g + 1) * rows, :]
        gw2 = lax.dot_general(gl, hid[...], (((1,), (0,)), ((), ())), preferred_element_type=F32)
        for i in range(group):
            a = g * group + i
            part_ref[ATOM * a : ATOM * (a + 1), :] = gw2[SLOT * i : SLOT * i + ATOM, :]
    part_ref[HEADS:W1_AT, :] = jnp.zeros((W1_AT - HEADS, HID), F32)

    pl.semaphore_wait(barrier, len(near))
    send = Sends(send_sem, recv_sem)
    waves, row, at = [], 0, 0
    for i, sizes in enumerate(WAVES):
        waves.append(Wave(i, sizes, row, me, core, send, part_ref, tot, buffers[8 * i : 8 * (i + 1)]))
        row += 2 * sum(sizes)
    assert row == TOTAL_ROWS
    wave0, wave1, wave2 = waves
    wave0.swap()

    for a in range(ACT):
        ga = glt[SLOT * a : SLOT * (a + 1), :].astype(F32)
        gb2[ATOM * a : ATOM * (a + 1), :] = jnp.broadcast_to(jnp.sum(ga, axis=1, keepdims=True), (SLOT, 128))[:ATOM]
    gb2[HEADS:, :] = jnp.zeros((1024 - HEADS, 128), F32)
    gb2_row = gb2[...].T[0:1, :]

    def back(t, gb1):
        cols = pl.ds(pl.multiple_of(t * 256, 256), 256)
        gh = lax.dot_general(glt[:, cols], w2p[...], (((0,), (0,)), ((), ())), preferred_element_type=F32)
        g16 = jnp.where(hid[cols, :].astype(F32) > 0.0, gh, 0.0).astype(BF16)
        gp[cols, :] = g16
        return gb1 + jnp.sum(g16.astype(F32), axis=0, keepdims=True)

    gb1 = lax.fori_loop(0, ROWS // 256, back, jnp.zeros((1, HID), F32))

    lane = lax.broadcasted_iota(jnp.int32, (1, HID), 1)
    top = jnp.max(top_row)
    loss = jnp.sum(loss_row)
    part_ref[B1_AT:, :] = jnp.concatenate(
        [
            gb1,
            gb2_row[:, :HID],
            gb2_row[:, HID:],
            jnp.where(lane == me, top, 0.0),
            jnp.where(lane == 0, loss, 0.0),
            jnp.zeros((TOTAL_ROWS - LOSS_AT - 1, HID), F32),
        ],
        axis=0,
    )

    def grad_w1(wave, half, tiles, size):
        low = wave.row + half * wave.half
        start = jnp.maximum(low - W1_AT, 0)
        span = jnp.minimum(low + wave.half - W1_AT, FEAT) - start

        def tile(i, carry):
            at = start + jnp.minimum(i * size, span - size)
            rows = pl.ds(pl.multiple_of(at, 16), size)
            out = pl.ds(pl.multiple_of(at + W1_AT, 16), size)
            part_ref[out, :] = jnp.dot(feat[rows, :], gp[...], preferred_element_type=F32)
            return carry

        lax.fori_loop(0, tiles, tile, 0)

    steps = [wave.steps() for wave in waves]

    def go(text):
        for digit in text:
            next(steps[int(digit)])

    go("0")
    grad_w1(wave1, 1 - core, 3, 256)
    wave1.swap()
    go("0")
    grad_w1(wave1, core, 3, 256)
    go("10")
    grad_w1(wave2, 1 - core, 4, 224)
    wave2.swap()
    go("01")
    grad_w1(wave2, core, 4, 224)
    go("2" + SCHEDULE)
    for copy in send.made:
        copy.wait_send()


def finish_kernel(
    tot, ce, w1_out, b1_out, w2_out, b2_out, loss_out, prio, w2_copy, sems,
):
    first = pltpu.make_async_copy(tot.at[W1_AT:B1_AT, :], w1_out, sems.at[0])
    first.start()
    w2_copy[...] = tot[:HEADS, :]
    second = pltpu.make_async_copy(w2_copy, w2_out, sems.at[1])
    second.start()
    b1_out[...] = tot[B1_AT : B1_AT + 1, :]
    b2_out[...] = jnp.concatenate([tot[B2_AT : B2_AT + 1, :], tot[B2_AT + 1 : B2_AT + 2, :]], axis=1)[:, :HEADS]
    loss_out[...] = tot[LOSS_AT : LOSS_AT + 1, 0:1] * (1.0 / (ROWS * 128))
    top = jnp.max(tot[TOP_AT : TOP_AT + 1, 0:128])
    prio[...] = ce[...] / jnp.maximum(top, 1.0)
    first.wait()
    second.wait()


SCHEDULE = "01201012012012121020212120122"


class Sends:
    def __init__(self, send_sem, recv_sem):
        self.send_sem, self.recv_sem, self.made = send_sem, recv_sem, []

    def __call__(self, src, dst, device):
        i = len(self.made)
        copy = pltpu.make_async_remote_copy(
            src_ref=src, dst_ref=dst, send_sem=self.send_sem.at[i], recv_sem=self.recv_sem.at[i],
            device_id=(device,), device_id_type=MESH,
        )
        copy.start()
        self.made.append(copy)
        return copy


COPIES = len(WAVES) * 3 * 38
LO, HI, ALL = slice(0, HID // 2), slice(HID // 2, HID), slice(0, HID)
ORDER = (2, 1, 3, 0)


def rows_at(start, size):
    return pl.ds(pl.multiple_of(start, 8), size)


def lanes_at(p):
    return pl.ds(pl.multiple_of(p * 128, 128), 128)


def ring(me, axis):
    stride = 32 - 33 * axis + 9 * axis * axis
    at = (me // stride) % 4
    return at, [me + stride * ((at + d) % 4 - at) for d in range(4)]


class Wave:
    def __init__(self, index, sizes, row, me, core, send, part, tot, buffers):
        self.row, self.half, self.send, self.part, self.tot = row, sum(sizes), send, part, tot
        self.work, self.plus_a, self.minus_a, self.one_a, self.plus_b, self.minus_b, self.one_b, self.piece = buffers
        self.sizes = sizes
        self.first = [sum(sizes[:s]) for s in range(3)]
        self.base = row + core * self.half
        self.other = row + (1 - core) * self.half
        self.sibling = me + 1 - 2 * core
        self.mine = [[ring(me, (s + k + core) % 3) for k in range(3)] for s in range(3)]
        self.theirs = [ring(me, (s + 1 - core) % 3)[0] for s in range(3)]

    def swap(self):
        self.swapped = {}
        for d in ORDER:
            for s in range(3):
                q = self.sizes[s] // 4
                at = (self.theirs[s] + d) % 4 * q + self.first[s]
                self.swapped[s, d] = self.send(
                    self.part.at[rows_at(self.other + at, q), :], self.work.at[rows_at(at, q), :], self.sibling
                )

    def scatter(self, k, blocks, sizes, plus, minus, one, first_stage):
        send, work = self.send, self.work
        copies, quarter = {}, {}
        for d in ORDER:
            for s in range(3):
                at, ahead = self.mine[s][k]
                q = sizes[s]
                local = blocks[s] + (at + d) % 4 * q
                rows = rows_at(local, q)
                quarter[s, d] = rows
                if first_stage:
                    self.swapped[s, d].wait_recv()
                    work[rows, :] = work[rows, :] + self.part[rows_at(self.base + local, q), :]
                here = pl.ds(0, q)
                if d == 2:
                    copies[s, "p1"] = send(work.at[rows, LO], one.at[s, here, LO], ahead[1])
                    copies[s, "m1"] = send(work.at[rows, HI], one.at[s, here, HI], ahead[3])
                elif d == 1:
                    copies[s, "p2"] = send(work.at[rows, HI], plus.at[s, here, HI], ahead[1])
                elif d == 3:
                    copies[s, "m2"] = send(work.at[rows, LO], minus.at[s, here, LO], ahead[3])
        yield
        for s in range(3):
            at, ahead = self.mine[s][k]
            here = pl.ds(0, sizes[s])
            copies[s, "p1"].wait_recv()
            rows = quarter[s, 1]
            work[rows, LO] = work[rows, LO] + one[s, here, LO]
            copies[s, "p3"] = send(work.at[rows, LO], plus.at[s, here, LO], ahead[1])
            copies[s, "m1"].wait_recv()
            rows = quarter[s, 3]
            work[rows, HI] = work[rows, HI] + one[s, here, HI]
            copies[s, "m3"] = send(work.at[rows, HI], minus.at[s, here, HI], ahead[3])
        yield
        for s in range(3):
            here = pl.ds(0, sizes[s])
            for name in ("p2", "m2", "p3", "m3"):
                copies[s, name].wait_recv()
            rows = quarter[s, 0]
            work[rows, :] = work[rows, :] + (plus[s, here, :] + minus[s, here, :])

    def gather(self, k, blocks, sizes, pair):
        copies, pairs = {}, []

        def put(s, d, lanes, device):
            start = self.base + blocks[s] + (self.mine[s][k][0] + d) % 4 * sizes[s]
            ref = self.tot.at[rows_at(start, sizes[s]), lanes]
            return self.send(ref, ref, device)

        def to_sibling(s, d):
            if pair:
                pairs.append(put(s, d, ALL, self.sibling))

        for s in range(3):
            ahead = self.mine[s][k][1]
            copies[s, "p1"] = put(s, 0, LO, ahead[1])
            copies[s, "m1"] = put(s, 0, HI, ahead[3])
            copies[s, "p2"] = put(s, 0, HI, ahead[1])
            copies[s, "m2"] = put(s, 0, LO, ahead[3])
        for s in range(3):
            to_sibling(s, 0)
        yield
        for s in range(3):
            ahead = self.mine[s][k][1]
            copies[s, "p1"].wait_recv()
            copies[s, "p3"] = put(s, 3, LO, ahead[1])
            copies[s, "m1"].wait_recv()
            copies[s, "m3"] = put(s, 1, HI, ahead[3])
        yield
        for s in range(3):
            copies[s, "p2"].wait_recv()
            to_sibling(s, 3)
            copies[s, "m2"].wait_recv()
            to_sibling(s, 1)
        for s in range(3):
            copies[s, "p3"].wait_recv()
            copies[s, "m3"].wait_recv()
            to_sibling(s, 2)
        if pair:
            yield
        for copy in pairs:
            copy.wait_recv()

    def steps(self):
        size_a = [size // 4 for size in self.sizes]
        size_b = [size // 16 for size in self.sizes]
        block_a = self.first
        yield from self.scatter(0, block_a, size_a, self.plus_a, self.minus_a, self.one_a, True)
        block_b = [block_a[s] + self.mine[s][0][0] * size_a[s] for s in range(3)]
        yield from self.scatter(1, block_b, size_b, self.plus_b, self.minus_b, self.one_b, False)
        block_c = [block_b[s] + self.mine[s][1][0] * size_b[s] for s in range(3)]

        piece, work, tot = self.piece, self.work, self.tot
        last, final = {}, {}
        for d in (2, 1, 3):
            for s in range(3):
                at, ahead = self.mine[s][2]
                last[s, d] = self.send(
                    work.at[rows_at(block_c[s], size_b[s]), lanes_at((at + d) % 4)],
                    piece.at[s, d - 1, pl.ds(0, size_b[s]), :], ahead[d],
                )
        yield
        for s in range(3):
            at, ahead = self.mine[s][2]
            here = pl.ds(0, size_b[s])
            for d in (1, 3, 2):
                last[s, d].wait_recv()
            got = work[rows_at(block_c[s], size_b[s]), lanes_at(at)] + (piece[s, 0, here, :] + piece[s, 2, here, :])
            rows = rows_at(self.base + block_c[s], size_b[s])
            tot[rows, lanes_at(at)] = got + piece[s, 1, here, :]
            for d in (2, 1, 3):
                ref = tot.at[rows, lanes_at(at)]
                final[s, d] = self.send(ref, ref, ahead[d])
        yield
        for s in range(3):
            for d in (1, 3, 2):
                final[s, d].wait_recv()
        yield from self.gather(1, block_b, size_b, False)
        yield from self.gather(0, block_a, size_a, True)
        yield


def wave_buffers(sizes):
    q, half = max(sizes) // 4, sum(sizes)
    return [
        pltpu.VMEM((half, HID), F32),
        pltpu.VMEM((3, q, HID), F32),
        pltpu.VMEM((3, q, HID), F32),
        pltpu.VMEM((3, q, HID), F32),
        pltpu.VMEM((3, q // 4, HID), F32),
        pltpu.VMEM((3, q // 4, HID), F32),
        pltpu.VMEM((3, q // 4, HID), F32),
        pltpu.VMEM((3, 3, q // 4, 128), F32),
    ]


def in_hbm(x):
    return pltpu.with_memory_space_constraint(x, pltpu.HBM)


def main(*args):
    hbm = pl.BlockSpec(memory_space=pltpu.HBM)
    vm = pl.BlockSpec(memory_space=pltpu.VMEM)
    buffers = []
    for sizes in WAVES:
        buffers += wave_buffers(sizes)
    return pl.pallas_call(
        main_kernel,
        name="gradients_and_sum",
        in_specs=[hbm] * 11,
        out_specs=[vm, vm],
        out_shape=[pltpu.VMEM((TOTAL_ROWS, HID), F32), pltpu.VMEM((1, ROWS), F32)],
        scratch_shapes=[
            pltpu.VMEM((FEAT, ROWS), BF16),
            pltpu.VMEM((FEAT, HID), BF16),
            pltpu.VMEM((1, HID), F32),
            pltpu.VMEM((HEADS, HID), BF16),
            pltpu.VMEM((1, HEADS), F32),
            pltpu.VMEM((1, ROWS), jnp.int32),
            pltpu.VMEM((ACT, ATOM, ROWS), F32),
            pltpu.VMEM((1, ROWS), jnp.int32),
            pltpu.VMEM((ATOM, ROWS), jnp.int32),
            pltpu.VMEM((ATOM, ROWS), F32),
            pltpu.VMEM((1, ROWS), F32),
            pltpu.VMEM((HEADS, HID), F32),
            pltpu.VMEM((HEAD, HID), BF16),
            pltpu.VMEM((1088, 128), F32),
            pltpu.VMEM((ATOM, 128), F32),
            pltpu.VMEM((ATOM, 128), F32),
            pltpu.VMEM((SLOT, ROWS), F32),
            pltpu.VMEM((ROWS, HID), BF16),
            pltpu.VMEM((HEAD, ROWS), BF16),
            pltpu.VMEM((ROWS, HID), BF16),
            pltpu.VMEM((1024, 128), F32),
            pltpu.VMEM((TOTAL_ROWS, HID), F32),
            pltpu.SemaphoreType.DMA((11,)),
            pltpu.SemaphoreType.DMA((COPIES,)),
            pltpu.SemaphoreType.DMA((COPIES,)),
            *buffers,
        ],
        compiler_params=pltpu.CompilerParams(
            vmem_limit_bytes=54 * 1024 * 1024, collective_id=0, has_side_effects=True
        ),
    )(*[in_hbm(x) for x in args])


def finish(tot, ce):
    hbm = pl.BlockSpec(memory_space=pltpu.HBM)
    vm = pl.BlockSpec(memory_space=pltpu.VMEM)
    return pl.pallas_call(
        finish_kernel,
        name="finish",
        in_specs=[vm, vm],
        out_specs=[hbm, vm, hbm, vm, vm, vm],
        out_shape=[
            jax.ShapeDtypeStruct((FEAT, HID), F32),
            jax.ShapeDtypeStruct((1, HID), F32),
            jax.ShapeDtypeStruct((HEADS, HID), F32),
            jax.ShapeDtypeStruct((1, HEADS), F32),
            jax.ShapeDtypeStruct((1, 1), F32),
            jax.ShapeDtypeStruct((1, ROWS), F32),
        ],
        scratch_shapes=[pltpu.VMEM((HEADS, HID), F32), pltpu.SemaphoreType.DMA((2,))],
        compiler_params=pltpu.CompilerParams(vmem_limit_bytes=8 * 1024 * 1024),
    )(tot, ce)


def on_device(features, w_one, b_one, w_two, b_two, action, target_probs, next_action, lower_idx, upper_frac, is_weight):
    tot, ce = main(
        features.T, w_one.T, b_one[None, :], w_two.T, b_two[None, :], action[None, :],
        target_probs.transpose(1, 2, 0), next_action[None, :], lower_idx.T, upper_frac.T, is_weight[None, :],
    )
    gw1, gb1, gw2, gb2, loss, prio = finish(tot, ce)
    return gw1.T, gb1[0], gw2.T, gb2[0], loss[0, 0], prio[0]


def solution(mesh):
    in_specs = (
        P("dp", None), P(), P(), P(), P(), P("dp"), P("dp", None, None), P("dp"), P("dp", None), P("dp", None), P("dp"),
    )
    out_specs = (P(), P(), P(), P(), P(), P("dp"))
    return jax.shard_map(on_device, mesh=mesh, in_specs=in_specs, out_specs=out_specs, check_vma=False)
```

time: 99.2 us -> 89.6 us (0.903)
  local copies, waits for them, and re-layouts: 12.5 us -> 0 us
  Pallas kernels: 84 us -> 88.6 us
  between operations: 2.45 us -> 0.64 us
    unnamed x17 -> x0, local copies, waits for them, and re-layouts: 6.49 us -> none
    transpose x2 -> x0, local copies, waits for them, and re-layouts: 4.87 us -> none  [the longest x1 3.47 us: on_device(): total[:FEAT]]
    pallas_call x2, Pallas kernels: 84 us -> 88.6 us  [the longest x1 84.7 us: main(): pl.pallas_call(main_kernel, name='gradients_and_sum', in_specs=[hbm] * 11...]
    slice x2 -> x0, local copies, waits for them, and re-layouts: 1.09 us -> none  [the longest x1 0.58 us: on_device(): total[B1_AT]]
where the time goes in v2:
time: 89.6 us; the launch traced here: 89.3 us
  Pallas kernels  88.6 us (99%)
    pallas_call x1, Pallas kernels, main(): pl.pallas_call(main_kernel, name='gradients_and_sum', in_specs=[hbm] * 11...  84.7 us
    pallas_call x1, Pallas kernels, finish(): pl.pallas_call(finish_kernel, name='finish', in_specs=[vm, vm], out_specs...  3.98 us

profile of v2, /device:TPU:1, one launch (start us, length us, event | category | flops | bytes accessed | tf_op | source)
XLA Modules:
  0.0 89.3 jit_solution(5410731449379401800)
XLA Ops:
  0.6 84.7 %gradients_and_sum.1 = (f32[4096,512]{1,0:T(8,128)S(1)}, f32[1,1024]{1,0:T(1,128)S(1)}) custom-call(bf16[3136,1024]{1,0:T(8,128)(2,1)} %bitcast.17, bf16[3136,512]{1,0:T(8,128)(2,1)} %bitcast.19, f32[1,512]{1,0:T(1,128)} %bitcast.27, bf16[918,512]{1,0:T(8,128)(2,1)} %bitcast.20, f32[1,918]{1,0:T(1,128)} %bitcast.23, s32[1,1024]{1,0:T(1,128)} %bitcast.24, ...), custom_call_target="tpu_custom_call" | custom-call | tf_op jit(solution)/shard_map/gradients_and_sum/pallas_call | solution.py:438
  85.3 4.0 %finish.1 = (f32[3136,512]{1,0:T(8,128)}, f32[1,512]{1,0:T(1,128)}, f32[918,512]{1,0:T(8,128)}, f32[1,918]{1,0:T(1,128)}, f32[1,1]{1,0:T(1,128)}, /*index=5*/f32[1,1024]{1,0:T(1,128)}) custom-call(f32[4096,512]{1,0:T(8,128)S(1)} %get-tuple-element.14.tot, f32[1,1024]{1,0:T(1,128)S(1)} %get-tuple-element.15.ce), custom_call_target="tpu_custom_call" | custom-call | tf_op jit(solution)/shard_map/finish/pallas_call | solution.py:481

commit v3 on v2

--- a/solution.py
+++ b/solution.py
@@ -139,10 +139,9 @@
     part_ref[HEADS:W1_AT, :] = jnp.zeros((W1_AT - HEADS, HID), F32)
 
     pl.semaphore_wait(barrier, len(near))
-    send = Sends(send_sem, recv_sem)
     waves, row, at = [], 0, 0
     for i, sizes in enumerate(WAVES):
-        waves.append(Wave(i, sizes, row, me, core, send, part_ref, tot, buffers[8 * i : 8 * (i + 1)]))
+        waves.append(Wave(i, sizes, row, me, core, send_sem, recv_sem, part_ref, tot, buffers[8 * i : 8 * (i + 1)]))
         row += 2 * sum(sizes)
     assert row == TOTAL_ROWS
     wave0, wave1, wave2 = waves
@@ -201,16 +200,14 @@
     go("0")
     grad_w1(wave1, 1 - core, 3, 256)
     wave1.swap()
-    go("0")
     grad_w1(wave1, core, 3, 256)
-    go("10")
     grad_w1(wave2, 1 - core, 4, 224)
     wave2.swap()
-    go("01")
+    go("1")
     grad_w1(wave2, core, 4, 224)
-    go("2" + SCHEDULE)
-    for copy in send.made:
-        copy.wait_send()
+    go(SCHEDULE)
+    for wave in waves:
+        wave.drain()
 
 
 def finish_kernel(
@@ -230,25 +227,10 @@
     second.wait()
 
 
-SCHEDULE = "01201012012012121020212120122"
-
-
-class Sends:
-    def __init__(self, send_sem, recv_sem):
-        self.send_sem, self.recv_sem, self.made = send_sem, recv_sem, []
-
-    def __call__(self, src, dst, device):
-        i = len(self.made)
-        copy = pltpu.make_async_remote_copy(
-            src_ref=src, dst_ref=dst, send_sem=self.send_sem.at[i], recv_sem=self.recv_sem.at[i],
-            device_id=(device,), device_id_type=MESH,
-        )
-        copy.start()
-        self.made.append(copy)
-        return copy
-
-
-COPIES = len(WAVES) * 3 * 38
+SCHEDULE = "0201021012012012012012120120122012"
+
+
+RECEIVES = 21
 LO, HI, ALL = slice(0, HID // 2), slice(HID // 2, HID), slice(0, HID)
 ORDER = (2, 1, 3, 0)
 
@@ -268,8 +250,8 @@
 
 
 class Wave:
-    def __init__(self, index, sizes, row, me, core, send, part, tot, buffers):
-        self.row, self.half, self.send, self.part, self.tot = row, sum(sizes), send, part, tot
+    def __init__(self, index, sizes, row, me, core, send_sem, recv_sem, part, tot, buffers):
+        self.row, self.half, self.part, self.tot = row, sum(sizes), part, tot
         self.work, self.plus_a, self.minus_a, self.one_a, self.plus_b, self.minus_b, self.one_b, self.piece = buffers
         self.sizes = sizes
         self.first = [sum(sizes[:s]) for s in range(3)]
@@ -278,21 +260,48 @@
         self.sibling = me + 1 - 2 * core
         self.mine = [[ring(me, (s + k + core) % 3) for k in range(3)] for s in range(3)]
         self.theirs = [ring(me, (s + 1 - core) % 3)[0] for s in range(3)]
+        self.send_sem = send_sem.at[index]
+        self.recv_sems = [recv_sem.at[index, i] for i in range(RECEIVES)]
+        self.sent = 0
+
+    def take(self):
+        return self.recv_sems.pop(0)
+
+    def send(self, src, dst, device, recv_sem):
+        self.sent += src.shape[0] * src.shape[1]
+        pltpu.make_async_remote_copy(
+            src_ref=src, dst_ref=dst, send_sem=self.send_sem, recv_sem=recv_sem,
+            device_id=(device,), device_id_type=MESH,
+        ).start()
+
+    def wait(self, sem, rows, lanes):
+        ref = self.part.at[0:rows, 0:lanes]
+        pltpu.make_async_copy(ref, ref, sem).wait()
+
+    def drain(self):
+        tiles = self.sent // 1024
+        self.wait(self.send_sem, tiles // 4 * 8, HID)
+        if tiles % 4:
+            self.wait(self.send_sem, 8, tiles % 4 * 128)
 
     def swap(self):
-        self.swapped = {}
+        self.swapped = {d: self.take() for d in ORDER}
         for d in ORDER:
             for s in range(3):
                 q = self.sizes[s] // 4
                 at = (self.theirs[s] + d) % 4 * q + self.first[s]
-                self.swapped[s, d] = self.send(
-                    self.part.at[rows_at(self.other + at, q), :], self.work.at[rows_at(at, q), :], self.sibling
+                self.send(
+                    self.part.at[rows_at(self.other + at, q), :], self.work.at[rows_at(at, q), :], self.sibling,
+                    self.swapped[d],
                 )
 
     def scatter(self, k, blocks, sizes, plus, minus, one, first_stage):
         send, work = self.send, self.work
-        copies, quarter = {}, {}
+        up, down, rest = self.take(), self.take(), self.take()
+        quarter = {}
         for d in ORDER:
+            if first_stage:
+                self.wait(self.swapped[d], sum(sizes), HID)
             for s in range(3):
                 at, ahead = self.mine[s][k]
                 q = sizes[s]
@@ -300,77 +309,60 @@
                 rows = rows_at(local, q)
                 quarter[s, d] = rows
                 if first_stage:
-                    self.swapped[s, d].wait_recv()
                     work[rows, :] = work[rows, :] + self.part[rows_at(self.base + local, q), :]
                 here = pl.ds(0, q)
                 if d == 2:
-                    copies[s, "p1"] = send(work.at[rows, LO], one.at[s, here, LO], ahead[1])
-                    copies[s, "m1"] = send(work.at[rows, HI], one.at[s, here, HI], ahead[3])
+                    send(work.at[rows, LO], one.at[s, here, LO], ahead[1], up)
+                    send(work.at[rows, HI], one.at[s, here, HI], ahead[3], down)
                 elif d == 1:
-                    copies[s, "p2"] = send(work.at[rows, HI], plus.at[s, here, HI], ahead[1])
+                    send(work.at[rows, HI], plus.at[s, here, HI], ahead[1], rest)
                 elif d == 3:
-                    copies[s, "m2"] = send(work.at[rows, LO], minus.at[s, here, LO], ahead[3])
-        yield
+                    send(work.at[rows, LO], minus.at[s, here, LO], ahead[3], rest)
+        yield
+        for name, d, lanes, target, step in ((up, 1, LO, plus, 1), (down, 3, HI, minus, 3)):
+            self.wait(name, sum(sizes), HID // 2)
+            for s in range(3):
+                rows, here = quarter[s, d], pl.ds(0, sizes[s])
+                work[rows, lanes] = work[rows, lanes] + one[s, here, lanes]
+                send(work.at[rows, lanes], target.at[s, here, lanes], self.mine[s][k][1][step], rest)
+        yield
+        self.wait(rest, 2 * sum(sizes), HID)
         for s in range(3):
-            at, ahead = self.mine[s][k]
-            here = pl.ds(0, sizes[s])
-            copies[s, "p1"].wait_recv()
-            rows = quarter[s, 1]
-            work[rows, LO] = work[rows, LO] + one[s, here, LO]
-            copies[s, "p3"] = send(work.at[rows, LO], plus.at[s, here, LO], ahead[1])
-            copies[s, "m1"].wait_recv()
-            rows = quarter[s, 3]
-            work[rows, HI] = work[rows, HI] + one[s, here, HI]
-            copies[s, "m3"] = send(work.at[rows, HI], minus.at[s, here, HI], ahead[3])
-        yield
-        for s in range(3):
-            here = pl.ds(0, sizes[s])
-            for name in ("p2", "m2", "p3", "m3"):
-                copies[s, name].wait_recv()
-            rows = quarter[s, 0]
+            rows, here = quarter[s, 0], pl.ds(0, sizes[s])
             work[rows, :] = work[rows, :] + (plus[s, here, :] + minus[s, here, :])
 
     def gather(self, k, blocks, sizes, pair):
-        copies, pairs = {}, []
-
-        def put(s, d, lanes, device):
+        up, down, rest, far = self.take(), self.take(), self.take(), self.take()
+        both = self.take() if pair else None
+
+        def put(s, d, lanes, device, sem):
             start = self.base + blocks[s] + (self.mine[s][k][0] + d) % 4 * sizes[s]
             ref = self.tot.at[rows_at(start, sizes[s]), lanes]
-            return self.send(ref, ref, device)
-
-        def to_sibling(s, d):
+            self.send(ref, ref, device, sem)
+
+        def to_sibling(*quarters):
             if pair:
-                pairs.append(put(s, d, ALL, self.sibling))
-
-        for s in range(3):
-            ahead = self.mine[s][k][1]
-            copies[s, "p1"] = put(s, 0, LO, ahead[1])
-            copies[s, "m1"] = put(s, 0, HI, ahead[3])
-            copies[s, "p2"] = put(s, 0, HI, ahead[1])
-            copies[s, "m2"] = put(s, 0, LO, ahead[3])
-        for s in range(3):
-            to_sibling(s, 0)
-        yield
-        for s in range(3):
-            ahead = self.mine[s][k][1]
-            copies[s, "p1"].wait_recv()
-            copies[s, "p3"] = put(s, 3, LO, ahead[1])
-            copies[s, "m1"].wait_recv()
-            copies[s, "m3"] = put(s, 1, HI, ahead[3])
-        yield
-        for s in range(3):
-            copies[s, "p2"].wait_recv()
-            to_sibling(s, 3)
-            copies[s, "m2"].wait_recv()
-            to_sibling(s, 1)
-        for s in range(3):
-            copies[s, "p3"].wait_recv()
-            copies[s, "m3"].wait_recv()
-            to_sibling(s, 2)
+                for s in range(3):
+                    for d in quarters:
+                        put(s, d, ALL, self.sibling, both)
+
+        for lanes, step, sem in ((LO, 1, up), (HI, 3, down), (HI, 1, rest), (LO, 3, rest)):
+            for s in range(3):
+                put(s, 0, lanes, self.mine[s][k][1][step], sem)
+        to_sibling(0)
+        yield
+        for sem, d, lanes, step in ((up, 3, LO, 1), (down, 1, HI, 3)):
+            self.wait(sem, sum(sizes), HID // 2)
+            for s in range(3):
+                put(s, d, lanes, self.mine[s][k][1][step], far)
+        yield
+        self.wait(rest, sum(sizes), HID)
+        to_sibling(3, 1)
+        self.wait(far, sum(sizes), HID)
+        to_sibling(2)
         if pair:
             yield
-        for copy in pairs:
-            copy.wait_recv()
+            self.wait(both, self.half, HID)
 
     def steps(self):
         size_a = [size // 4 for size in self.sizes]
@@ -382,30 +374,27 @@
         block_c = [block_b[s] + self.mine[s][1][0] * size_b[s] for s in range(3)]
 
         piece, work, tot = self.piece, self.work, self.tot
-        last, final = {}, {}
+        last, final = self.take(), self.take()
         for d in (2, 1, 3):
             for s in range(3):
                 at, ahead = self.mine[s][2]
-                last[s, d] = self.send(
+                self.send(
                     work.at[rows_at(block_c[s], size_b[s]), lanes_at((at + d) % 4)],
-                    piece.at[s, d - 1, pl.ds(0, size_b[s]), :], ahead[d],
+                    piece.at[s, d - 1, pl.ds(0, size_b[s]), :], ahead[d], last,
                 )
         yield
+        self.wait(last, 3 * sum(size_b), 128)
         for s in range(3):
             at, ahead = self.mine[s][2]
             here = pl.ds(0, size_b[s])
-            for d in (1, 3, 2):
-                last[s, d].wait_recv()
             got = work[rows_at(block_c[s], size_b[s]), lanes_at(at)] + (piece[s, 0, here, :] + piece[s, 2, here, :])
             rows = rows_at(self.base + block_c[s], size_b[s])
             tot[rows, lanes_at(at)] = got + piece[s, 1, here, :]
             for d in (2, 1, 3):
                 ref = tot.at[rows, lanes_at(at)]
-                final[s, d] = self.send(ref, ref, ahead[d])
-        yield
-        for s in range(3):
-            for d in (1, 3, 2):
-                final[s, d].wait_recv()
+                self.send(ref, ref, ahead[d], final)
+        yield
+        self.wait(final, 3 * sum(size_b), 128)
         yield from self.gather(1, block_b, size_b, False)
         yield from self.gather(0, block_a, size_a, True)
         yield
@@ -465,8 +454,8 @@
             pltpu.VMEM((1024, 128), F32),
             pltpu.VMEM((TOTAL_ROWS, HID), F32),
             pltpu.SemaphoreType.DMA((11,)),
-            pltpu.SemaphoreType.DMA((COPIES,)),
-            pltpu.SemaphoreType.DMA((COPIES,)),
+            pltpu.SemaphoreType.DMA((len(WAVES),)),
+            pltpu.SemaphoreType.DMA((len(WAVES), RECEIVES)),
             *buffers,
         ],
         compiler_params=pltpu.CompilerParams(

time: 89.6 us -> 81.5 us (0.910)
  Pallas kernels: 88.6 us -> 80.7 us
    pallas_call x1, Pallas kernels: 84.7 us -> 76.7 us  [main(): pl.pallas_call(main_kernel, name='gradients_and_sum', in_specs=[hbm] * 11...]
where the time goes in v3:
time: 81.5 us; the launch traced here: 81.4 us
  Pallas kernels  80.7 us (99%)
    pallas_call x1, Pallas kernels, main(): pl.pallas_call(main_kernel, name='gradients_and_sum', in_specs=[hbm] * 11...  76.7 us
    pallas_call x1, Pallas kernels, finish(): pl.pallas_call(finish_kernel, name='finish', in_specs=[vm, vm], out_specs...  3.98 us

profile of v3, /device:TPU:1, one launch (start us, length us, event | category | flops | bytes accessed | tf_op | source)
XLA Modules:
  0.0 81.4 jit_solution(13322936075446827861)
XLA Ops:
  0.6 76.7 %gradients_and_sum.1 = (f32[4096,512]{1,0:T(8,128)S(1)}, f32[1,1024]{1,0:T(1,128)S(1)}) custom-call(bf16[3136,1024]{1,0:T(8,128)(2,1)} %bitcast.17, bf16[3136,512]{1,0:T(8,128)(2,1)} %bitcast.19, f32[1,512]{1,0:T(1,128)} %bitcast.27, bf16[918,512]{1,0:T(8,128)(2,1)} %bitcast.20, f32[1,918]{1,0:T(1,128)} %bitcast.23, s32[1,1024]{1,0:T(1,128)} %bitcast.24, ...), custom_call_target="tpu_custom_call" | custom-call | tf_op jit(solution)/shard_map/gradients_and_sum/pallas_call | solution.py:427
  77.4 4.0 %finish.1 = (f32[3136,512]{1,0:T(8,128)}, f32[1,512]{1,0:T(1,128)}, f32[918,512]{1,0:T(8,128)}, f32[1,918]{1,0:T(1,128)}, f32[1,1]{1,0:T(1,128)}, /*index=5*/f32[1,1024]{1,0:T(1,128)}) custom-call(f32[4096,512]{1,0:T(8,128)S(1)} %get-tuple-element.14.tot, f32[1,1024]{1,0:T(1,128)S(1)} %get-tuple-element.15.ce), custom_call_target="tpu_custom_call" | custom-call | tf_op jit(solution)/shard_map/finish/pallas_call | solution.py:470

commit v4 on v3

--- a/solution.py
+++ b/solution.py
@@ -21,7 +21,13 @@
 TOP_AT = B2_AT + 2
 LOSS_AT = TOP_AT + 1
 TOTAL_ROWS = 4096
-WAVES = ((128, 128, 128), (256, 256, 256), (256, 256, 384))
+WAVES = (
+    ((128, 128, 128), None),
+    ((256, 256, 128), (3, 224)),
+    ((256, 128, 256), (3, 224)),
+    ((128, 128, 128), (2, 192)),
+)
+PLAN = "0aA0b1Bc02C12031230123102310321320312031233021"
 
 
 def main_kernel(
@@ -140,12 +146,11 @@
 
     pl.semaphore_wait(barrier, len(near))
     waves, row, at = [], 0, 0
-    for i, sizes in enumerate(WAVES):
-        waves.append(Wave(i, sizes, row, me, core, send_sem, recv_sem, part_ref, tot, buffers[8 * i : 8 * (i + 1)]))
+    for i, (sizes, _) in enumerate(WAVES):
+        waves.append(Wave(i, sizes, row, me, core, send_sem, recv_sem, part_ref, tot, buffers[6 * i : 6 * (i + 1)]))
         row += 2 * sum(sizes)
     assert row == TOTAL_ROWS
-    wave0, wave1, wave2 = waves
-    wave0.swap()
+    waves[0].swap()
 
     for a in range(ACT):
         ga = glt[SLOT * a : SLOT * (a + 1), :].astype(F32)
@@ -193,19 +198,15 @@
 
     steps = [wave.steps() for wave in waves]
 
-    def go(text):
-        for digit in text:
-            next(steps[int(digit)])
-
-    go("0")
-    grad_w1(wave1, 1 - core, 3, 256)
-    wave1.swap()
-    grad_w1(wave1, core, 3, 256)
-    grad_w1(wave2, 1 - core, 4, 224)
-    wave2.swap()
-    go("1")
-    grad_w1(wave2, core, 4, 224)
-    go(SCHEDULE)
+    for token in PLAN:
+        i = "0ABCD".find(token.upper())
+        if i > 0:
+            other = token.islower()
+            grad_w1(waves[i], 1 - core if other else core, *WAVES[i][1])
+            if other:
+                waves[i].swap()
+        else:
+            next(steps[int(token)])
     for wave in waves:
         wave.drain()
 
@@ -213,24 +214,24 @@
 def finish_kernel(
     tot, ce, w1_out, b1_out, w2_out, b2_out, loss_out, prio, w2_copy, sems,
 ):
-    first = pltpu.make_async_copy(tot.at[W1_AT:B1_AT, :], w1_out, sems.at[0])
-    first.start()
+    copies = []
+    for i in range(7):
+        rows = pl.ds(448 * i, 448)
+        copies.append(pltpu.make_async_copy(tot.at[pl.ds(W1_AT + 448 * i, 448), :], w1_out.at[rows, :], sems.at[i]))
+        copies[i].start()
     w2_copy[...] = tot[:HEADS, :]
-    second = pltpu.make_async_copy(w2_copy, w2_out, sems.at[1])
-    second.start()
+    copies.append(pltpu.make_async_copy(w2_copy, w2_out, sems.at[7]))
+    copies[7].start()
     b1_out[...] = tot[B1_AT : B1_AT + 1, :]
     b2_out[...] = jnp.concatenate([tot[B2_AT : B2_AT + 1, :], tot[B2_AT + 1 : B2_AT + 2, :]], axis=1)[:, :HEADS]
     loss_out[...] = tot[LOSS_AT : LOSS_AT + 1, 0:1] * (1.0 / (ROWS * 128))
     top = jnp.max(tot[TOP_AT : TOP_AT + 1, 0:128])
     prio[...] = ce[...] / jnp.maximum(top, 1.0)
-    first.wait()
-    second.wait()
-
-
-SCHEDULE = "0201021012012012012012120120122012"
-
-
-RECEIVES = 21
+    for copy in copies:
+        copy.wait()
+
+
+RECEIVES = 16
 LO, HI, ALL = slice(0, HID // 2), slice(HID // 2, HID), slice(0, HID)
 ORDER = (2, 1, 3, 0)
 
@@ -252,7 +253,7 @@
 class Wave:
     def __init__(self, index, sizes, row, me, core, send_sem, recv_sem, part, tot, buffers):
         self.row, self.half, self.part, self.tot = row, sum(sizes), part, tot
-        self.work, self.plus_a, self.minus_a, self.one_a, self.plus_b, self.minus_b, self.one_b, self.piece = buffers
+        self.work, self.plus, self.minus, self.one, self.whole, self.piece = buffers
         self.sizes = sizes
         self.first = [sum(sizes[:s]) for s in range(3)]
         self.base = row + core * self.half
@@ -295,21 +296,19 @@
                     self.swapped[d],
                 )
 
-    def scatter(self, k, blocks, sizes, plus, minus, one, first_stage):
-        send, work = self.send, self.work
+    def scatter(self, blocks, sizes):
+        k, send, work, plus, minus, one = 0, self.send, self.work, self.plus, self.minus, self.one
         up, down, rest = self.take(), self.take(), self.take()
         quarter = {}
         for d in ORDER:
-            if first_stage:
-                self.wait(self.swapped[d], sum(sizes), HID)
+            self.wait(self.swapped[d], sum(sizes), HID)
             for s in range(3):
                 at, ahead = self.mine[s][k]
                 q = sizes[s]
                 local = blocks[s] + (at + d) % 4 * q
                 rows = rows_at(local, q)
                 quarter[s, d] = rows
-                if first_stage:
-                    work[rows, :] = work[rows, :] + self.part[rows_at(self.base + local, q), :]
+                work[rows, :] = work[rows, :] + self.part[rows_at(self.base + local, q), :]
                 here = pl.ds(0, q)
                 if d == 2:
                     send(work.at[rows, LO], one.at[s, here, LO], ahead[1], up)
@@ -331,46 +330,65 @@
             rows, here = quarter[s, 0], pl.ds(0, sizes[s])
             work[rows, :] = work[rows, :] + (plus[s, here, :] + minus[s, here, :])
 
-    def gather(self, k, blocks, sizes, pair):
-        up, down, rest, far = self.take(), self.take(), self.take(), self.take()
-        both = self.take() if pair else None
-
-        def put(s, d, lanes, device, sem):
-            start = self.base + blocks[s] + (self.mine[s][k][0] + d) % 4 * sizes[s]
-            ref = self.tot.at[rows_at(start, sizes[s]), lanes]
-            self.send(ref, ref, device, sem)
+    def scatter_straight(self, blocks, sizes):
+        whole, work, sem = self.whole, self.work, self.take()
+        for d in (2, 1, 3):
+            for s in range(3):
+                at, ahead = self.mine[s][1]
+                rows = rows_at(blocks[s] + (at + d) % 4 * sizes[s], sizes[s])
+                self.send(work.at[rows, ALL], whole.at[s, d - 1, pl.ds(0, sizes[s]), :], ahead[d], sem)
+        yield
+        self.wait(sem, 3 * sum(sizes), HID)
+        for s in range(3):
+            rows, here = rows_at(blocks[s] + self.mine[s][1][0] * sizes[s], sizes[s]), pl.ds(0, sizes[s])
+            work[rows, :] = (work[rows, :] + whole[s, 1, here, :]) + (whole[s, 0, here, :] + whole[s, 2, here, :])
+
+    def put(self, k, blocks, sizes, s, d, lanes, device, sem):
+        start = self.base + blocks[s] + (self.mine[s][k][0] + d) % 4 * sizes[s]
+        ref = self.tot.at[rows_at(start, sizes[s]), lanes]
+        self.send(ref, ref, device, sem)
+
+    def gather_straight(self, blocks, sizes):
+        sem = self.take()
+        for d in (2, 1, 3):
+            for s in range(3):
+                self.put(1, blocks, sizes, s, 0, ALL, self.mine[s][1][1][d], sem)
+        yield
+        self.wait(sem, 3 * sum(sizes), HID)
+
+    def gather(self, blocks, sizes):
+        up, down, rest, far, both = self.take(), self.take(), self.take(), self.take(), self.take()
+        put = functools.partial(self.put, 0, blocks, sizes)
 
         def to_sibling(*quarters):
-            if pair:
-                for s in range(3):
-                    for d in quarters:
-                        put(s, d, ALL, self.sibling, both)
+            for s in range(3):
+                for d in quarters:
+                    put(s, d, ALL, self.sibling, both)
 
         for lanes, step, sem in ((LO, 1, up), (HI, 3, down), (HI, 1, rest), (LO, 3, rest)):
             for s in range(3):
-                put(s, 0, lanes, self.mine[s][k][1][step], sem)
+                put(s, 0, lanes, self.mine[s][0][1][step], sem)
         to_sibling(0)
         yield
         for sem, d, lanes, step in ((up, 3, LO, 1), (down, 1, HI, 3)):
             self.wait(sem, sum(sizes), HID // 2)
             for s in range(3):
-                put(s, d, lanes, self.mine[s][k][1][step], far)
+                put(s, d, lanes, self.mine[s][0][1][step], far)
         yield
         self.wait(rest, sum(sizes), HID)
         to_sibling(3, 1)
         self.wait(far, sum(sizes), HID)
         to_sibling(2)
-        if pair:
-            yield
-            self.wait(both, self.half, HID)
+        yield
+        self.wait(both, self.half, HID)
 
     def steps(self):
         size_a = [size // 4 for size in self.sizes]
         size_b = [size // 16 for size in self.sizes]
         block_a = self.first
-        yield from self.scatter(0, block_a, size_a, self.plus_a, self.minus_a, self.one_a, True)
+        yield from self.scatter(block_a, size_a)
         block_b = [block_a[s] + self.mine[s][0][0] * size_a[s] for s in range(3)]
-        yield from self.scatter(1, block_b, size_b, self.plus_b, self.minus_b, self.one_b, False)
+        yield from self.scatter_straight(block_b, size_b)
         block_c = [block_b[s] + self.mine[s][1][0] * size_b[s] for s in range(3)]
 
         piece, work, tot = self.piece, self.work, self.tot
@@ -395,8 +413,8 @@
                 self.send(ref, ref, ahead[d], final)
         yield
         self.wait(final, 3 * sum(size_b), 128)
-        yield from self.gather(1, block_b, size_b, False)
-        yield from self.gather(0, block_a, size_a, True)
+        yield from self.gather_straight(block_b, size_b)
+        yield from self.gather(block_a, size_a)
         yield
 
 
@@ -407,9 +425,7 @@
         pltpu.VMEM((3, q, HID), F32),
         pltpu.VMEM((3, q, HID), F32),
         pltpu.VMEM((3, q, HID), F32),
-        pltpu.VMEM((3, q // 4, HID), F32),
-        pltpu.VMEM((3, q // 4, HID), F32),
-        pltpu.VMEM((3, q // 4, HID), F32),
+        pltpu.VMEM((3, 3, q // 4, HID), F32),
         pltpu.VMEM((3, 3, q // 4, 128), F32),
     ]
 
@@ -422,7 +438,7 @@
     hbm = pl.BlockSpec(memory_space=pltpu.HBM)
     vm = pl.BlockSpec(memory_space=pltpu.VMEM)
     buffers = []
-    for sizes in WAVES:
+    for sizes, _ in WAVES:
         buffers += wave_buffers(sizes)
     return pl.pallas_call(
         main_kernel,
@@ -480,7 +496,7 @@
             jax.ShapeDtypeStruct((1, 1), F32),
             jax.ShapeDtypeStruct((1, ROWS), F32),
         ],
-        scratch_shapes=[pltpu.VMEM((HEADS, HID), F32), pltpu.SemaphoreType.DMA((2,))],
+        scratch_shapes=[pltpu.VMEM((HEADS, HID), F32), pltpu.SemaphoreType.DMA((8,))],
         compiler_params=pltpu.CompilerParams(vmem_limit_bytes=8 * 1024 * 1024),
     )(tot, ce)
 

time: 81.5 us -> 74.4 us (0.913)
  Pallas kernels: 80.7 us -> 73.7 us
    pallas_call x1, Pallas kernels: 76.7 us -> 69.7 us  [main(): pl.pallas_call(main_kernel, name='gradients_and_sum', in_specs=[hbm] * 11...]
where the time goes in v4:
time: 74.4 us; the launch traced here: 74.3 us
  Pallas kernels  73.7 us (99%)
    pallas_call x1, Pallas kernels, main(): pl.pallas_call(main_kernel, name='gradients_and_sum', in_specs=[hbm] * 11...  69.7 us
    pallas_call x1, Pallas kernels, finish(): pl.pallas_call(finish_kernel, name='finish', in_specs=[vm, vm], out_specs...  3.99 us

profile of v4, /device:TPU:1, one launch (start us, length us, event | category | flops | bytes accessed | tf_op | source)
XLA Modules:
  0.0 74.3 jit_solution(5536226846864005063)
XLA Ops:
  0.6 69.7 %gradients_and_sum.1 = (f32[4096,512]{1,0:T(8,128)S(1)}, f32[1,1024]{1,0:T(1,128)S(1)}) custom-call(bf16[3136,1024]{1,0:T(8,128)(2,1)} %bitcast.17, bf16[3136,512]{1,0:T(8,128)(2,1)} %bitcast.19, f32[1,512]{1,0:T(1,128)} %bitcast.27, bf16[918,512]{1,0:T(8,128)(2,1)} %bitcast.20, f32[1,918]{1,0:T(1,128)} %bitcast.23, s32[1,1024]{1,0:T(1,128)} %bitcast.24, ...), custom_call_target="tpu_custom_call" | custom-call | tf_op jit(solution)/shard_map/gradients_and_sum/pallas_call | solution.py:443
  70.3 4.0 %finish.1 = (f32[3136,512]{1,0:T(8,128)}, f32[1,512]{1,0:T(1,128)}, f32[918,512]{1,0:T(8,128)}, f32[1,918]{1,0:T(1,128)}, f32[1,1]{1,0:T(1,128)}, /*index=5*/f32[1,1024]{1,0:T(1,128)}) custom-call(f32[4096,512]{1,0:T(8,128)S(1)} %get-tuple-element.14.tot, f32[1,1024]{1,0:T(1,128)S(1)} %get-tuple-element.15.ce), custom_call_target="tpu_custom_call" | custom-call | tf_op jit(solution)/shard_map/finish/pallas_call | solution.py:486

commit v5 on v4

--- a/solution.py
+++ b/solution.py
@@ -23,11 +23,11 @@
 TOTAL_ROWS = 4096
 WAVES = (
     ((128, 128, 128), None),
-    ((256, 256, 128), (3, 224)),
-    ((256, 128, 256), (3, 224)),
-    ((128, 128, 128), (2, 192)),
+    ((256, 128, 128), (2, 256)),
+    ((128, 256, 128), (2, 256)),
+    ((256, 128, 256), (2, 320)),
 )
-PLAN = "0aA0b1Bc02C12031230123102310321320312031233021"
+PLAN = "0aAb1B02c1C03102310231203120312301231201320323"
 
 
 def main_kernel(
@@ -39,12 +39,14 @@
     me = lax.axis_index("dp")
     core = me % 2
     sibling = me + 1 - 2 * core
+    left, right = slice(0, ROWS // 2), slice(ROWS // 2, ROWS)
     pairs = [
         (w2_hbm, w2raw), (b2_hbm, b2_ref), (nact_hbm, nact_ref), (low_hbm, low_ref), (frac_hbm, frac_ref),
-        (tp_hbm, tp), (w1_hbm, w1), (b1_hbm, b1_ref), (feat_hbm, feat), (act_hbm, act_ref), (isw_hbm, isw_ref),
+        (tp_hbm, tp), (b1_hbm, b1_ref), (act_hbm, act_ref), (isw_hbm, isw_ref),
+        (w1_hbm, w1), (feat_hbm.at[:, left], feat.at[:, left]), (feat_hbm.at[:, right], feat.at[:, right]),
     ]
     copies = [pltpu.make_async_copy(src, dst, sems.at[i]) for i, (src, dst) in enumerate(pairs)]
-    for copy in copies:
+    for copy in copies[:9]:
         copy.start()
     near = [sibling]
     for axis in range(3):
@@ -54,6 +56,8 @@
         pl.semaphore_signal(barrier, inc=1, device_id=(device,), device_id_type=MESH)
 
     copies[0].wait()
+    for copy in copies[9:]:
+        copy.start()
     copies[1].wait()
     w2f[...] = w2raw[...].astype(F32)
     wrow = lax.broadcasted_iota(jnp.int32, (SLOT, HID), 0)
@@ -69,7 +73,8 @@
 
     for copy in copies[2:6]:
         copy.wait()
-    atom_row = lax.broadcasted_iota(jnp.int32, (SLOT, 128), 0)
+    atom_row = lax.broadcasted_iota(jnp.int32, (56, 128), 0)
+    proj[56:, :] = jnp.zeros((SLOT - 56, ROWS), F32)
 
     def project(t, carry):
         lanes = pl.ds(pl.multiple_of(t * 128, 128), 128)
@@ -80,34 +85,32 @@
         frac = frac_ref[:, lanes]
         mlow[...] = probs * (1.0 - frac)
         mhigh[...] = probs * frac
-        low_sum = jnp.zeros((SLOT, 128), F32)
-        high_sum = jnp.zeros((SLOT, 128), F32)
+        low_sum = jnp.zeros((56, 128), F32)
+        high_sum = jnp.zeros((56, 128), F32)
         for j in range(ATOM):
             hot = low_ref[pl.ds(j, 1), lanes] == atom_row
             low_sum = low_sum + jnp.where(hot, mlow[pl.ds(j, 1), :], 0.0)
             high_sum = high_sum + jnp.where(hot, mhigh[pl.ds(j, 1), :], 0.0)
         high_sum = jnp.where(atom_row == 0, 0.0, pltpu.roll(high_sum, 1, 0))
-        proj[:, lanes] = low_sum + high_sum
+        proj[0:56, lanes] = low_sum + high_sum
         return carry
 
     lax.fori_loop(0, ROWS // 128, project, 0)
 
-    for copy in copies[6:]:
+    for copy in copies[6:10]:
         copy.wait()
 
-    def forward(t, carry):
-        cols = pl.ds(pl.multiple_of(t * 256, 256), 256)
+    for t in range(2):
+        copies[10 + t].wait()
+        cols = slice(512 * t, 512 * (t + 1))
         pre = lax.dot_general(feat[:, cols], w1[...], (((0,), (0,)), ((), ())), preferred_element_type=F32)
         hid[cols, :] = jnp.maximum(pre + b1_ref[...], 0.0).astype(BF16)
-        return carry
-
-    lax.fori_loop(0, ROWS // 256, forward, 0)
 
     valid = lax.broadcasted_iota(jnp.int32, (SLOT, 256), 0) < ATOM
 
     def head(t, carry):
         loss, top = carry
-        cols = pl.ds(pl.multiple_of(t * 256, 256), 256)
+        cols = slice(256 * t, 256 * (t + 1))
         logits = lax.dot_general(w2p[...], hid[cols, :], (((1,), (1,)), ((), ())), preferred_element_type=F32)
         action = act_ref[:, cols]
         chosen = jnp.zeros((SLOT, 256), F32)
@@ -130,9 +133,10 @@
         ce_ref[:, cols] = cross
         return loss + weight * cross, jnp.maximum(top, cross)
 
-    loss_row, top_row = lax.fori_loop(
-        0, ROWS // 256, head, (jnp.zeros((1, 256), F32), jnp.full((1, 256), -jnp.inf, F32))
-    )
+    carry = (jnp.zeros((1, 256), F32), jnp.full((1, 256), -jnp.inf, F32))
+    for t in range(ROWS // 256):
+        carry = head(t, carry)
+    loss_row, top_row = carry
 
     group = 6
     for g in range(ACT // group):
@@ -159,13 +163,13 @@
     gb2_row = gb2[...].T[0:1, :]
 
     def back(t, gb1):
-        cols = pl.ds(pl.multiple_of(t * 256, 256), 256)
+        cols = pl.ds(pl.multiple_of(t * 512, 512), 512)
         gh = lax.dot_general(glt[:, cols], w2p[...], (((0,), (0,)), ((), ())), preferred_element_type=F32)
         g16 = jnp.where(hid[cols, :].astype(F32) > 0.0, gh, 0.0).astype(BF16)
         gp[cols, :] = g16
         return gb1 + jnp.sum(g16.astype(F32), axis=0, keepdims=True)
 
-    gb1 = lax.fori_loop(0, ROWS // 256, back, jnp.zeros((1, HID), F32))
+    gb1 = lax.fori_loop(0, ROWS // 512, back, jnp.zeros((1, HID), F32))
 
     lane = lax.broadcasted_iota(jnp.int32, (1, HID), 1)
     top = jnp.max(top_row)
@@ -212,21 +216,27 @@
 
 
 def finish_kernel(
-    tot, ce, w1_out, b1_out, w2_out, b2_out, loss_out, prio, w2_copy, sems,
+    tot, ce, w1_out, b1_out, w2_out, b2_out, loss_out, prio_out, w2_copy, b1_copy, b2_copy, loss_copy, prio_copy, sems,
 ):
     copies = []
-    for i in range(7):
-        rows = pl.ds(448 * i, 448)
-        copies.append(pltpu.make_async_copy(tot.at[pl.ds(W1_AT + 448 * i, 448), :], w1_out.at[rows, :], sems.at[i]))
-        copies[i].start()
+
+    def copy_out(src, dst):
+        copies.append(pltpu.make_async_copy(src, dst, sems.at[len(copies)]))
+        copies[-1].start()
+
     w2_copy[...] = tot[:HEADS, :]
-    copies.append(pltpu.make_async_copy(w2_copy, w2_out, sems.at[7]))
-    copies[7].start()
-    b1_out[...] = tot[B1_AT : B1_AT + 1, :]
-    b2_out[...] = jnp.concatenate([tot[B2_AT : B2_AT + 1, :], tot[B2_AT + 1 : B2_AT + 2, :]], axis=1)[:, :HEADS]
-    loss_out[...] = tot[LOSS_AT : LOSS_AT + 1, 0:1] * (1.0 / (ROWS * 128))
+    copy_out(w2_copy, w2_out)
+    for i in range(4):
+        copy_out(tot.at[pl.ds(W1_AT + 784 * i, 784), :], w1_out.at[pl.ds(784 * i, 784), :])
+    b1_copy[...] = tot[B1_AT : B1_AT + 1, :]
+    copy_out(b1_copy, b1_out)
+    b2_copy[...] = jnp.concatenate([tot[B2_AT : B2_AT + 1, :], tot[B2_AT + 1 : B2_AT + 2, :]], axis=1)[:, :HEADS]
+    copy_out(b2_copy, b2_out)
+    loss_copy[...] = tot[LOSS_AT : LOSS_AT + 1, 0:1] * (1.0 / (ROWS * 128))
+    copy_out(loss_copy, loss_out)
     top = jnp.max(tot[TOP_AT : TOP_AT + 1, 0:128])
-    prio[...] = ce[...] / jnp.maximum(top, 1.0)
+    prio_copy[...] = ce[...] / jnp.maximum(top, 1.0)
+    copy_out(prio_copy, prio_out)
     for copy in copies:
         copy.wait()
 
@@ -469,7 +479,7 @@
             pltpu.VMEM((ROWS, HID), BF16),
             pltpu.VMEM((1024, 128), F32),
             pltpu.VMEM((TOTAL_ROWS, HID), F32),
-            pltpu.SemaphoreType.DMA((11,)),
+            pltpu.SemaphoreType.DMA((12,)),
             pltpu.SemaphoreType.DMA((len(WAVES),)),
             pltpu.SemaphoreType.DMA((len(WAVES), RECEIVES)),
             *buffers,
@@ -487,7 +497,7 @@
         finish_kernel,
         name="finish",
         in_specs=[vm, vm],
-        out_specs=[hbm, vm, hbm, vm, vm, vm],
+        out_specs=[hbm] * 6,
         out_shape=[
             jax.ShapeDtypeStruct((FEAT, HID), F32),
             jax.ShapeDtypeStruct((1, HID), F32),
@@ -496,7 +506,14 @@
             jax.ShapeDtypeStruct((1, 1), F32),
             jax.ShapeDtypeStruct((1, ROWS), F32),
         ],
-        scratch_shapes=[pltpu.VMEM((HEADS, HID), F32), pltpu.SemaphoreType.DMA((8,))],
+        scratch_shapes=[
+            pltpu.VMEM((HEADS, HID), F32),
+            pltpu.VMEM((1, HID), F32),
+            pltpu.VMEM((1, HEADS), F32),
+            pltpu.VMEM((1, 1), F32),
+            pltpu.VMEM((1, ROWS), F32),
+            pltpu.SemaphoreType.DMA((9,)),
+        ],
         compiler_params=pltpu.CompilerParams(vmem_limit_bytes=8 * 1024 * 1024),
     )(tot, ce)
 

time: 74.4 us -> 69.6 us (0.935)
  Pallas kernels: 73.7 us -> 68.8 us
    pallas_call x1, Pallas kernels: 69.7 us -> 65.3 us  [main(): pl.pallas_call(main_kernel, name='gradients_and_sum', in_specs=[hbm] * 11...]
where the time goes in v5:
time: 69.6 us; the launch traced here: 69.5 us
  Pallas kernels  68.8 us (99%)
    pallas_call x1, Pallas kernels, main(): pl.pallas_call(main_kernel, name='gradients_and_sum', in_specs=[hbm] * 11...  65.3 us
    pallas_call x1, Pallas kernels, finish(): pl.pallas_call(finish_kernel, name='finish', in_specs=[vm, vm], out_specs...  3.53 us

profile of v5, /device:TPU:1, one launch (start us, length us, event | category | flops | bytes accessed | tf_op | source)
XLA Modules:
  0.0 69.5 jit_solution(13880589184004347284)
XLA Ops:
  0.6 65.3 %gradients_and_sum.1 = (f32[4096,512]{1,0:T(8,128)S(1)}, f32[1,1024]{1,0:T(1,128)S(1)}) custom-call(bf16[3136,1024]{1,0:T(8,128)(2,1)} %bitcast.17, bf16[3136,512]{1,0:T(8,128)(2,1)} %bitcast.19, f32[1,512]{1,0:T(1,128)} %bitcast.27, bf16[918,512]{1,0:T(8,128)(2,1)} %bitcast.20, f32[1,918]{1,0:T(1,128)} %bitcast.23, s32[1,1024]{1,0:T(1,128)} %bitcast.24, ...), custom_call_target="tpu_custom_call" | custom-call | tf_op jit(solution)/shard_map/gradients_and_sum/pallas_call | solution.py:453
  66.0 3.5 %finish.1 = (f32[3136,512]{1,0:T(8,128)}, f32[1,512]{1,0:T(1,128)}, f32[918,512]{1,0:T(8,128)}, f32[1,918]{1,0:T(1,128)}, f32[1,1]{1,0:T(1,128)}, /*index=5*/f32[1,1024]{1,0:T(1,128)}) custom-call(f32[4096,512]{1,0:T(8,128)S(1)} %get-tuple-element.14.tot, f32[1,1024]{1,0:T(1,128)S(1)} %get-tuple-element.15.ce), custom_call_target="tpu_custom_call" | custom-call | tf_op jit(solution)/shard_map/finish/pallas_call | solution.py:496

commit v6 on v5

--- a/solution.py
+++ b/solution.py
@@ -24,10 +24,10 @@
 WAVES = (
     ((128, 128, 128), None),
     ((256, 128, 128), (2, 256)),
-    ((128, 256, 128), (2, 256)),
-    ((256, 128, 256), (2, 320)),
+    ((256, 256, 256), (2, 384)),
+    ((128, 128, 128), (2, 192)),
 )
-PLAN = "0aAb1B02c1C03102310231203120312301231201320323"
+PLAN = "a0A1b0B12c0C1230123012301230132103203213230132"
 
 
 def main_kernel(
@@ -40,13 +40,16 @@
     core = me % 2
     sibling = me + 1 - 2 * core
     left, right = slice(0, ROWS // 2), slice(ROWS // 2, ROWS)
-    pairs = [
-        (w2_hbm, w2raw), (b2_hbm, b2_ref), (nact_hbm, nact_ref), (low_hbm, low_ref), (frac_hbm, frac_ref),
-        (tp_hbm, tp), (b1_hbm, b1_ref), (act_hbm, act_ref), (isw_hbm, isw_ref),
+    pairs = [(nact_hbm, nact_ref), (low_hbm, low_ref), (frac_hbm, frac_ref)]
+    for t in range(4):
+        cols = slice(256 * t, 256 * (t + 1))
+        pairs.append((tp_hbm.at[:, :, cols], tp.at[:, :, cols]))
+    pairs += [
+        (w2_hbm, w2raw), (b2_hbm, b2_ref), (b1_hbm, b1_ref), (act_hbm, act_ref), (isw_hbm, isw_ref),
         (w1_hbm, w1), (feat_hbm.at[:, left], feat.at[:, left]), (feat_hbm.at[:, right], feat.at[:, right]),
     ]
     copies = [pltpu.make_async_copy(src, dst, sems.at[i]) for i, (src, dst) in enumerate(pairs)]
-    for copy in copies[:9]:
+    for copy in copies[:7]:
         copy.start()
     near = [sibling]
     for axis in range(3):
@@ -55,24 +58,10 @@
     for device in near:
         pl.semaphore_signal(barrier, inc=1, device_id=(device,), device_id_type=MESH)
 
-    copies[0].wait()
-    for copy in copies[9:]:
+    for copy in copies[:4]:
+        copy.wait()
+    for copy in copies[7:]:
         copy.start()
-    copies[1].wait()
-    w2f[...] = w2raw[...].astype(F32)
-    wrow = lax.broadcasted_iota(jnp.int32, (SLOT, HID), 0)
-    for a in range(ACT):
-        if a < ACT - 1:
-            block = w2f[ATOM * a : ATOM * a + SLOT, :]
-        else:
-            block = jnp.concatenate([w2f[ATOM * a : HEADS, :], jnp.zeros((SLOT - ATOM, HID), F32)], axis=0)
-        w2p[SLOT * a : SLOT * (a + 1), :] = jnp.where(wrow < ATOM, block, 0.0).astype(BF16)
-    b2row = jnp.concatenate([b2_ref[...], jnp.zeros((1, 1024 - HEADS), F32)], axis=1)
-    b2col[0:1024, :] = jnp.broadcast_to(b2row, (128, 1024)).T
-    b2col[1024:, :] = jnp.zeros((64, 128), F32)
-
-    for copy in copies[2:6]:
-        copy.wait()
     atom_row = lax.broadcasted_iota(jnp.int32, (56, 128), 0)
     proj[56:, :] = jnp.zeros((SLOT - 56, ROWS), F32)
 
@@ -95,13 +84,30 @@
         proj[0:56, lanes] = low_sum + high_sum
         return carry
 
-    lax.fori_loop(0, ROWS // 128, project, 0)
-
-    for copy in copies[6:10]:
+    lax.fori_loop(0, 2, project, 0)
+    for t in range(1, 4):
+        copies[3 + t].wait()
+        lax.fori_loop(2 * t, 2 * t + 2, project, 0)
+
+    copies[7].wait()
+    copies[8].wait()
+    w2f[...] = w2raw[...].astype(F32)
+    wrow = lax.broadcasted_iota(jnp.int32, (SLOT, HID), 0)
+    for a in range(ACT):
+        if a < ACT - 1:
+            block = w2f[ATOM * a : ATOM * a + SLOT, :]
+        else:
+            block = jnp.concatenate([w2f[ATOM * a : HEADS, :], jnp.zeros((SLOT - ATOM, HID), F32)], axis=0)
+        w2p[SLOT * a : SLOT * (a + 1), :] = jnp.where(wrow < ATOM, block, 0.0).astype(BF16)
+    b2row = jnp.concatenate([b2_ref[...], jnp.zeros((1, 1024 - HEADS), F32)], axis=1)
+    b2col[0:1024, :] = jnp.broadcast_to(b2row, (128, 1024)).T
+    b2col[1024:, :] = jnp.zeros((64, 128), F32)
+
+    for copy in copies[9:13]:
         copy.wait()
 
     for t in range(2):
-        copies[10 + t].wait()
+        copies[13 + t].wait()
         cols = slice(512 * t, 512 * (t + 1))
         pre = lax.dot_general(feat[:, cols], w1[...], (((0,), (0,)), ((), ())), preferred_element_type=F32)
         hid[cols, :] = jnp.maximum(pre + b1_ref[...], 0.0).astype(BF16)
@@ -156,12 +162,6 @@
     assert row == TOTAL_ROWS
     waves[0].swap()
 
-    for a in range(ACT):
-        ga = glt[SLOT * a : SLOT * (a + 1), :].astype(F32)
-        gb2[ATOM * a : ATOM * (a + 1), :] = jnp.broadcast_to(jnp.sum(ga, axis=1, keepdims=True), (SLOT, 128))[:ATOM]
-    gb2[HEADS:, :] = jnp.zeros((1024 - HEADS, 128), F32)
-    gb2_row = gb2[...].T[0:1, :]
-
     def back(t, gb1):
         cols = pl.ds(pl.multiple_of(t * 512, 512), 512)
         gh = lax.dot_general(glt[:, cols], w2p[...], (((0,), (0,)), ((), ())), preferred_element_type=F32)
@@ -171,21 +171,6 @@
 
     gb1 = lax.fori_loop(0, ROWS // 512, back, jnp.zeros((1, HID), F32))
 
-    lane = lax.broadcasted_iota(jnp.int32, (1, HID), 1)
-    top = jnp.max(top_row)
-    loss = jnp.sum(loss_row)
-    part_ref[B1_AT:, :] = jnp.concatenate(
-        [
-            gb1,
-            gb2_row[:, :HID],
-            gb2_row[:, HID:],
-            jnp.where(lane == me, top, 0.0),
-            jnp.where(lane == 0, loss, 0.0),
-            jnp.zeros((TOTAL_ROWS - LOSS_AT - 1, HID), F32),
-        ],
-        axis=0,
-    )
-
     def grad_w1(wave, half, tiles, size):
         low = wave.row + half * wave.half
         start = jnp.maximum(low - W1_AT, 0)
@@ -200,12 +185,35 @@
 
         lax.fori_loop(0, tiles, tile, 0)
 
+    def tail_rows():
+        for a in range(ACT):
+            ga = glt[SLOT * a : SLOT * (a + 1), :].astype(F32)
+            gb2[ATOM * a : ATOM * (a + 1), :] = jnp.broadcast_to(jnp.sum(ga, axis=1, keepdims=True), (SLOT, 128))[:ATOM]
+        gb2[HEADS:, :] = jnp.zeros((1024 - HEADS, 128), F32)
+        gb2_row = gb2[...].T[0:1, :]
+        lane = lax.broadcasted_iota(jnp.int32, (1, HID), 1)
+        top = jnp.max(top_row)
+        loss = jnp.sum(loss_row)
+        part_ref[B1_AT:, :] = jnp.concatenate(
+            [
+                gb1,
+                gb2_row[:, :HID],
+                gb2_row[:, HID:],
+                jnp.where(lane == me, top, 0.0),
+                jnp.where(lane == 0, loss, 0.0),
+                jnp.zeros((TOTAL_ROWS - LOSS_AT - 1, HID), F32),
+            ],
+            axis=0,
+        )
+
     steps = [wave.steps() for wave in waves]
 
     for token in PLAN:
         i = "0ABCD".find(token.upper())
         if i > 0:
             other = token.islower()
+            if other and i == len(waves) - 1:
+                tail_rows()
             grad_w1(waves[i], 1 - core if other else core, *WAVES[i][1])
             if other:
                 waves[i].swap()
@@ -479,7 +487,7 @@
             pltpu.VMEM((ROWS, HID), BF16),
             pltpu.VMEM((1024, 128), F32),
             pltpu.VMEM((TOTAL_ROWS, HID), F32),
-            pltpu.SemaphoreType.DMA((12,)),
+            pltpu.SemaphoreType.DMA((15,)),
             pltpu.SemaphoreType.DMA((len(WAVES),)),
             pltpu.SemaphoreType.DMA((len(WAVES), RECEIVES)),
             *buffers,

time: 69.6 us -> 68.6 us (0.986)
  Pallas kernels: 68.8 us -> 67.9 us
    pallas_call x1, Pallas kernels: 65.3 us -> 64.3 us  [main(): pl.pallas_call(main_kernel, name='gradients_and_sum', in_specs=[hbm] * 11...]
where the time goes in v6:
time: 68.6 us; the launch traced here: 68.5 us
  Pallas kernels  67.9 us (99%)
    pallas_call x1, Pallas kernels, main(): pl.pallas_call(main_kernel, name='gradients_and_sum', in_specs=[hbm] * 11...  64.3 us
    pallas_call x1, Pallas kernels, finish(): pl.pallas_call(finish_kernel, name='finish', in_specs=[vm, vm], out_specs...  3.53 us

profile of v6, /device:TPU:1, one launch (start us, length us, event | category | flops | bytes accessed | tf_op | source)
XLA Modules:
  0.0 68.5 jit_solution(114421231824773538)
XLA Ops:
  0.6 64.3 %gradients_and_sum.1 = (f32[4096,512]{1,0:T(8,128)S(1)}, f32[1,1024]{1,0:T(1,128)S(1)}) custom-call(bf16[3136,1024]{1,0:T(8,128)(2,1)} %bitcast.17, bf16[3136,512]{1,0:T(8,128)(2,1)} %bitcast.19, f32[1,512]{1,0:T(1,128)} %bitcast.27, bf16[918,512]{1,0:T(8,128)(2,1)} %bitcast.20, f32[1,918]{1,0:T(1,128)} %bitcast.23, s32[1,1024]{1,0:T(1,128)} %bitcast.24, ...), custom_call_target="tpu_custom_call" | custom-call | tf_op jit(solution)/shard_map/gradients_and_sum/pallas_call | solution.py:461
  65.0 3.5 %finish.1 = (f32[3136,512]{1,0:T(8,128)}, f32[1,512]{1,0:T(1,128)}, f32[918,512]{1,0:T(8,128)}, f32[1,918]{1,0:T(1,128)}, f32[1,1]{1,0:T(1,128)}, /*index=5*/f32[1,1024]{1,0:T(1,128)}) custom-call(f32[4096,512]{1,0:T(8,128)S(1)} %get-tuple-element.14.tot, f32[1,1024]{1,0:T(1,128)S(1)} %get-tuple-element.15.ce), custom_call_target="tpu_custom_call" | custom-call | tf_op jit(solution)/shard_map/finish/pallas_call | solution.py:504

commit v7 on v6

--- a/solution.py
+++ b/solution.py
@@ -232,10 +232,10 @@
         copies.append(pltpu.make_async_copy(src, dst, sems.at[len(copies)]))
         copies[-1].start()
 
+    for i in range(4):
+        copy_out(tot.at[pl.ds(W1_AT + 784 * i, 784), :], w1_out.at[pl.ds(784 * i, 784), :])
     w2_copy[...] = tot[:HEADS, :]
     copy_out(w2_copy, w2_out)
-    for i in range(4):
-        copy_out(tot.at[pl.ds(W1_AT + 784 * i, 784), :], w1_out.at[pl.ds(784 * i, 784), :])
     b1_copy[...] = tot[B1_AT : B1_AT + 1, :]
     copy_out(b1_copy, b1_out)
     b2_copy[...] = jnp.concatenate([tot[B2_AT : B2_AT + 1, :], tot[B2_AT + 1 : B2_AT + 2, :]], axis=1)[:, :HEADS]

time: 68.6 us -> 68.5 us (level)
  no operation moved by 1% of the time
where the time goes in v7:
time: 68.5 us; the launch traced here: 68.4 us
  Pallas kernels  67.7 us (99%)
    pallas_call x1, Pallas kernels, main(): pl.pallas_call(main_kernel, name='gradients_and_sum', in_specs=[hbm] * 11...  64.3 us
    pallas_call x1, Pallas kernels, finish(): pl.pallas_call(finish_kernel, name='finish', in_specs=[vm, vm], out_specs...  3.4 us

profile of v7, /device:TPU:1, one launch (start us, length us, event | category | flops | bytes accessed | tf_op | source)
XLA Modules:
  0.0 68.4 jit_solution(7760187648521423298)
XLA Ops:
  0.6 64.3 %gradients_and_sum.1 = (f32[4096,512]{1,0:T(8,128)S(1)}, f32[1,1024]{1,0:T(1,128)S(1)}) custom-call(bf16[3136,1024]{1,0:T(8,128)(2,1)} %bitcast.17, bf16[3136,512]{1,0:T(8,128)(2,1)} %bitcast.19, f32[1,512]{1,0:T(1,128)} %bitcast.27, bf16[918,512]{1,0:T(8,128)(2,1)} %bitcast.20, f32[1,918]{1,0:T(1,128)} %bitcast.23, s32[1,1024]{1,0:T(1,128)} %bitcast.24, ...), custom_call_target="tpu_custom_call" | custom-call | tf_op jit(solution)/shard_map/gradients_and_sum/pallas_call | solution.py:461
  65.0 3.4 %finish.1 = (f32[3136,512]{1,0:T(8,128)}, f32[1,512]{1,0:T(1,128)}, f32[918,512]{1,0:T(8,128)}, f32[1,918]{1,0:T(1,128)}, f32[1,1]{1,0:T(1,128)}, /*index=5*/f32[1,1024]{1,0:T(1,128)}) custom-call(f32[4096,512]{1,0:T(8,128)S(1)} %get-tuple-element.14.tot, f32[1,1024]{1,0:T(1,128)S(1)} %get-tuple-element.15.ce), custom_call_target="tpu_custom_call" | custom-call | tf_op jit(solution)/shard_map/finish/pallas_call | solution.py:504

commit v8 on v7

--- a/solution.py
+++ b/solution.py
@@ -91,13 +91,11 @@
 
     copies[7].wait()
     copies[8].wait()
-    w2f[...] = w2raw[...].astype(F32)
+    w2f[912:, :] = jnp.zeros((24, HID), F32)
+    w2f[:HEADS, :] = w2raw[...].astype(F32)
     wrow = lax.broadcasted_iota(jnp.int32, (SLOT, HID), 0)
     for a in range(ACT):
-        if a < ACT - 1:
-            block = w2f[ATOM * a : ATOM * a + SLOT, :]
-        else:
-            block = jnp.concatenate([w2f[ATOM * a : HEADS, :], jnp.zeros((SLOT - ATOM, HID), F32)], axis=0)
+        block = w2f[ATOM * a : ATOM * a + SLOT, :]
         w2p[SLOT * a : SLOT * (a + 1), :] = jnp.where(wrow < ATOM, block, 0.0).astype(BF16)
     b2row = jnp.concatenate([b2_ref[...], jnp.zeros((1, 1024 - HEADS), F32)], axis=1)
     b2col[0:1024, :] = jnp.broadcast_to(b2row, (128, 1024)).T
@@ -476,7 +474,7 @@
             pltpu.VMEM((ATOM, ROWS), jnp.int32),
             pltpu.VMEM((ATOM, ROWS), F32),
             pltpu.VMEM((1, ROWS), F32),
-            pltpu.VMEM((HEADS, HID), F32),
+            pltpu.VMEM((936, HID), F32),
             pltpu.VMEM((HEAD, HID), BF16),
             pltpu.VMEM((1088, 128), F32),
             pltpu.VMEM((ATOM, 128), F32),

time: 68.5 us -> 68.5 us (level)
  no operation moved by 1% of the time
where the time goes in v8:
time: 68.5 us; the launch traced here: 68.4 us
  Pallas kernels  67.7 us (99%)
    pallas_call x1, Pallas kernels, main(): pl.pallas_call(main_kernel, name='gradients_and_sum', in_specs=[hbm] * 11...  64.3 us
    pallas_call x1, Pallas kernels, finish(): pl.pallas_call(finish_kernel, name='finish', in_specs=[vm, vm], out_specs...  3.4 us

profile of v8, /device:TPU:1, one launch (start us, length us, event | category | flops | bytes accessed | tf_op | source)
XLA Modules:
  0.0 68.4 jit_solution(12514190401085773770)
XLA Ops:
  0.6 64.3 %gradients_and_sum.1 = (f32[4096,512]{1,0:T(8,128)S(1)}, f32[1,1024]{1,0:T(1,128)S(1)}) custom-call(bf16[3136,1024]{1,0:T(8,128)(2,1)} %bitcast.17, bf16[3136,512]{1,0:T(8,128)(2,1)} %bitcast.19, f32[1,512]{1,0:T(1,128)} %bitcast.27, bf16[918,512]{1,0:T(8,128)(2,1)} %bitcast.20, f32[1,918]{1,0:T(1,128)} %bitcast.23, s32[1,1024]{1,0:T(1,128)} %bitcast.24, ...), custom_call_target="tpu_custom_call" | custom-call | tf_op jit(solution)/shard_map/gradients_and_sum/pallas_call | solution.py:459
  65.0 3.4 %finish.1 = (f32[3136,512]{1,0:T(8,128)}, f32[1,512]{1,0:T(1,128)}, f32[918,512]{1,0:T(8,128)}, f32[1,918]{1,0:T(1,128)}, f32[1,1]{1,0:T(1,128)}, /*index=5*/f32[1,1024]{1,0:T(1,128)}) custom-call(f32[4096,512]{1,0:T(8,128)S(1)} %get-tuple-element.14.tot, f32[1,1024]{1,0:T(1,128)S(1)} %get-tuple-element.15.ce), custom_call_target="tpu_custom_call" | custom-call | tf_op jit(solution)/shard_map/finish/pallas_call | solution.py:502
